TPU v7x, 32 devices: a whole 2x2x4 slice. The times are simulated.
32 devices in a mesh: rows: 2 (over y), cols: 4 (over z), slabs: 2 (over x), trial: 2 (over core).
Axes of the slice: x: 2, y: 2, z: 4, core: 2. Of those that a mesh axis runs over, the one named last changes fastest.
Arguments:
- field_values: float32 [64, 16, 256, 128], P(('trial', 'rows'), 'cols', 'slabs'), parts along dimension 0, may hold values from 0.5 to 2
- conductance: float32 [64, 16, 256, 128], P(('trial', 'rows'), 'cols', 'slabs'), parts along dimension 0, may hold values from 0.03 to 0.15
- source: float32 [64, 16, 256, 128], P(('trial', 'rows'), 'cols', 'slabs'), parts along dimension 0, may hold values from -0.2 to 0.2
Outputs:
- anomaly: float32 [64, 16, 256, 128], P(('trial', 'rows'), 'cols', 'slabs'), parts along dimension 0
- field_values_end: float32 [64, 16, 256, 128], P(('trial', 'rows'), 'cols', 'slabs'), parts along dimension 0
There are 2 independent parts, one for each index of `trial`. A program takes and returns all parts, laid end to end along the dimension named above; each array names one. Nothing has to cross between parts.
All inputs are finite; a program needn't handle non-finite values.
Results may differ from a plain program's by a relative error of at most 0.00002.
Values sent between devices are 32-bit elements; how exact they have to be, the bound alone decides.
No kernel may reach another device: no remote copies, remote signals or barrier semaphores. Data moves between devices by JAX's collectives and lax.ppermute only.
A program may use at most 128 MiB of HBM per device.

v0:
```python
import jax
import jax.numpy as jnp
from jax import lax
from jax.experimental import pallas as pl
from jax.experimental.pallas import tpu as pltpu
from jax.sharding import PartitionSpec as P


STEPS = 4
CHUNKS = (9, 7)
LAST_CUT = (5, 2)
ROWS = 8
HBM = pl.BlockSpec(memory_space=pltpu.HBM)
VMEM = pl.BlockSpec(memory_space=pltpu.VMEM)
F32 = jnp.float32


def vmem(*shape):
    return pltpu.VMEM(shape, F32)


def call(body, ins, in_specs, outs, out_specs, scratch=(), aliases=None, flops=0):
    return pl.pallas_call(
        body,
        in_specs=in_specs,
        out_shape=outs,
        out_specs=out_specs,
        scratch_shapes=scratch,
        input_output_aliases=aliases or {},
        compiler_params=pltpu.CompilerParams(vmem_limit_bytes=12 * 2**20),
        cost_estimate=pl.CostEstimate(flops=flops, bytes_accessed=0, transcendentals=0) if flops else None,
    )(*ins)


def ports_of(axis):
    return (0,) if lax.axis_size(axis) == 2 else (0, 1)


def exchange(buffers, axis):
    count = lax.axis_size(axis)
    received = []
    for port, buffer in zip(ports_of(axis), buffers):
        perm = []
        for i in range(port, count - 1, 2):
            perm += [(i, i + 1), (i + 1, i)]
        received.append(lax.ppermute(buffer, axis, perm))
    return received


def is_upper(axis, port):
    odd = lax.axis_index(axis) % 2
    return odd if port == 0 else 1 - odd


def sent_index(axis, port, extent):
    return (1 - is_upper(axis, port)) * (extent - 1)


def halo_readers(axis, refs):
    upper = is_upper(axis, 0)
    if len(refs) == 1:
        has_lower = upper.astype(F32)
        has_upper = (1 - upper).astype(F32)
        return (lambda where: refs[0][where] * has_lower), (lambda where: refs[0][where] * has_upper)
    return (
        lambda where: jnp.where(upper == 1, refs[0][where], refs[1][where]),
        lambda where: jnp.where(upper == 1, refs[1][where], refs[0][where]),
    )


def run_copies(copies):
    for copy in copies:
        copy.start()
    for copy in copies:
        copy.wait()


def write_copies(cells, out, layers, first, rows, sems):
    return [
        pltpu.make_async_copy(cells.at[:, n], out.at[:, i, pl.ds(first, rows)], sems.at[n]) for n, i in enumerate(layers)
    ]


def cut_faces(field, z_spans, y_spans, with_x):
    J, I, K, L = field.shape
    z_ports, y_ports, x_ports = ports_of("cols"), ports_of("rows"), ports_of("slabs") if with_x else ()
    shapes = [vmem(J, kc, L) for _, kc in z_spans for _ in z_ports]
    shapes += [vmem(I, kc, L) for _, kc in y_spans for _ in y_ports]
    shapes += [vmem(J, I, L) for _ in x_ports]

    def body(u, *refs):
        sources = [u.at[:, sent_index("cols", port, I), pl.ds(k0, kc)] for k0, kc in z_spans for port in z_ports]
        sources += [u.at[sent_index("rows", port, J), :, pl.ds(k0, kc)] for k0, kc in y_spans for port in y_ports]
        sources += [u.at[:, :, sent_index("slabs", port, K)] for port in x_ports]
        run_copies([pltpu.make_async_copy(src, refs[n], refs[-1].at[n]) for n, src in enumerate(sources)])

    field = pltpu.with_memory_space_constraint(field, pltpu.HBM)
    outs = list(call(body, [field], [HBM], shapes, [VMEM] * len(shapes), [pltpu.SemaphoreType.DMA((len(shapes),))]))
    z = [[outs.pop(0) for _ in z_ports] for _ in z_spans]
    y = [[outs.pop(0) for _ in y_ports] for _ in y_spans]
    return z, y, outs


def stage(arrays):
    def body(*refs):
        n = len(arrays)
        run_copies([pltpu.make_async_copy(refs[m], refs[n + m], refs[-1].at[m]) for m in range(n)])

    held = [pltpu.with_memory_space_constraint(array, pltpu.HBM) for array in arrays]
    shapes = [vmem(*array.shape) for array in arrays]
    return call(body, held, [HBM] * len(held), shapes, [VMEM] * len(held), [pltpu.SemaphoreType.DMA((len(held),))])


def step(pieces, fields, cond, src, y_in, x_in, layers, z_spans, x_head, last, write=None):
    J, I, K, L = cond.shape
    nl = len(layers)
    z_ports, y_ports, x_ports = ports_of("cols"), ports_of("rows"), ports_of("slabs")
    first = pieces[0][1]
    rows = sum(piece[2] for piece in pieces)
    ins, slots = [], {}

    def add(array):
        if id(array) not in slots:
            slots[id(array)] = len(ins)
            ins.append(array)
        return slots[id(array)]

    cond_at, src_at = add(cond), add(src)
    near = {q + d for q, *_ in pieces for d in (-1, 0, 1)} & set(range(len(fields)))
    field_at = {q: add(fields[q][0]) for q in sorted(near)}
    z_at = [[add(array) for array in piece[3]] for piece in pieces]
    y_at = {q: [add(array) for array in y_in[q][0]] for q, *_ in pieces}
    x_at = [add(array) for array in x_in]
    head_at = add(x_head) if x_head is not None else None
    if write is not None:
        done, done_layers, (done_first, done_rows), buffer = write
        done_at = add(done)
        buffers = [] if buffer is None else [buffer]

    def body(*refs):
        if write is not None:
            copies = write_copies(refs[done_at], refs[-2], done_layers, done_first, done_rows, refs[-1])
            for copy in copies:
                copy.start()
            compute(refs[: len(ins)] + refs[len(ins) + len(buffers) : -2])
            for copy in copies:
                copy.wait()
        else:
            compute(refs)

    def compute(refs):
        outs = list(refs[len(ins) :])
        c, s = refs[cond_at], refs[src_at]
        out = outs.pop(0)
        if last:
            stats = outs.pop(0)
        else:
            z_out = [[outs.pop(0) for _ in z_ports] for _ in z_spans]
            y_out = [outs.pop(0) for _ in y_ports]
            x_out = [outs.pop(0) for _ in x_ports] if x_head is not None else []
        x_lo, x_hi = halo_readers("slabs", [refs[n] for n in x_at])
        sublane = lax.broadcasted_iota(jnp.int32, (ROWS, L), 0)

        def tile(k, q, z, z_first, z_to, z_to_first, at_low, at_high):
            u, base = refs[field_at[q]], fields[q][1]
            y_lo, y_hi = halo_readers("rows", [refs[n] for n in y_at[q]])
            if z:
                z_lo, z_hi = halo_readers("cols", z)
            in_y = pl.ds(k - y_in[q][1], ROWS)
            in_z = pl.ds(k - z_first, ROWS)
            here = pl.ds(k - first, ROWS)
            there = pl.ds(k, ROWS)
            known = {}

            def cells(j, i):
                if (j, i) not in known:
                    if j < 0:
                        known[j, i] = y_lo((i, in_y))
                    elif j >= J:
                        known[j, i] = y_hi((i, in_y))
                    elif i < 0:
                        known[j, i] = z_lo((j, in_z))
                    elif i >= I:
                        known[j, i] = z_hi((j, in_z))
                    else:
                        known[j, i] = u[j, i, pl.ds(k - base, ROWS)]
                return known[j, i]

            def edge_row(near_q, j, i, row):
                array, start = refs[field_at[near_q]], fields[near_q][1]
                return jnp.broadcast_to(array[j, i, pl.ds(row - start, 1)], (ROWS, L))

            def k_lower(j, i):
                if not at_low:
                    return u[j, i, pl.ds(k - base - 1, ROWS)]
                if q > 0:
                    edge = edge_row(q - 1, j, i, k - 1)
                else:
                    edge = jnp.broadcast_to(x_lo((j, pl.ds(i, 1))), (ROWS, L))
                return jnp.where(sublane == 0, edge, pltpu.roll(cells(j, i), 1, 0))

            def k_upper(j, i):
                if not at_high:
                    return u[j, i, pl.ds(k - base + 1, ROWS)]
                if q + 1 < len(fields):
                    edge = edge_row(q + 1, j, i, k + ROWS)
                else:
                    edge = jnp.broadcast_to(x_hi((j, pl.ds(i, 1))), (ROWS, L))
                return jnp.where(sublane == ROWS - 1, edge, pltpu.roll(cells(j, i), ROWS - 1, 0))

            totals = [None] * nl
            for j in range(J):
                for n, i in enumerate(layers):
                    middle = cells(j, i)
                    spread = (
                        (cells(j - 1, i) + cells(j + 1, i))
                        + (cells(j, i - 1) + cells(j, i + 1))
                        + (k_lower(j, i) + k_upper(j, i))
                        - 6.0 * middle
                    )
                    new = middle + c[j, i, there] * spread + s[j, i, there]
                    out[j, n, here] = new
                    if last:
                        totals[n] = new if j == 0 else totals[n] + new
                    if i == 0:
                        lowest = new
                    if i == I - 1:
                        highest = new
                if not last:
                    for ref, port in zip(z_to, z_ports):
                        ref[j, pl.ds(k - z_to_first, ROWS)] = jnp.where(is_upper("cols", port) == 1, lowest, highest)
                for at in list(known):
                    if at[0] < j:
                        del known[at]
            if last:
                for n in range(nl):
                    mean = totals[n] * (1.0 / J)
                    spread = None
                    for j in range(J):
                        off = out[j, n, here] - mean
                        spread = off * off if j == 0 else spread + off * off
                    stats[0, n, here] = mean
                    stats[1, n, here] = spread

        for (q, k0, kc, _), z_refs in zip(pieces, z_at):
            z = [refs[n] for n in z_refs]
            array_low, array_high = fields[q][1], fields[q][1] + fields[q][0].shape[2]
            targets = [(0, K, None)] if last else [(*span, n) for n, span in enumerate(z_spans)]
            for t0, tc, n in targets:
                low, high = max(k0, t0), min(k0 + kc, t0 + tc)
                if low >= high:
                    continue
                z_to = z_out[n] if n is not None else []
                same = (q, z, k0, z_to, t0)
                begin, end = low, high
                if low == array_low:
                    tile(low, *same, True, low + ROWS == array_high)
                    begin += ROWS
                if high == array_high and begin < high:
                    tile(high - ROWS, *same, False, True)
                    end -= ROWS
                if begin < end:

                    def inner(t, carry, same=same):
                        tile(pl.multiple_of(t * ROWS, ROWS), *same, False, False)
                        return carry

                    lax.fori_loop(begin // ROWS, end // ROWS, inner, 0)
        if not last:
            for ref, port in zip(y_out, y_ports):
                ref[...] = out[sent_index("rows", port, J)]
            for ref, port in zip(x_out, x_ports):
                for j in range(J):
                    head = refs[head_at][j, :, 0, :]
                    tail = out[j, :, rows - 1, :]
                    upper = is_upper("slabs", port).astype(F32)
                    ref[j] = head * upper + tail * (1.0 - upper)

    shapes = [vmem(J, nl, rows, L)]
    if last:
        shapes.append(vmem(2, nl, rows, L))
    else:
        for _, tc in z_spans:
            shapes += [vmem(J, tc, L)] * len(z_ports)
        shapes += [vmem(I, rows, L)] * len(y_ports)
        if x_head is not None:
            shapes += [vmem(J, I, L)] * len(x_ports)
    all_ins, in_specs, out_specs, scratch, aliases = ins, [VMEM] * len(ins), [VMEM] * len(shapes), [], None
    if write is not None:
        all_ins, in_specs = ins + buffers, in_specs + [HBM] * len(buffers)
        aliases = {len(ins): len(shapes)} if buffers else None
        shapes, out_specs = shapes + [jax.ShapeDtypeStruct(cond.shape, F32)], out_specs + [HBM]
        scratch = [pltpu.SemaphoreType.DMA((len(done_layers),))]
    outs = list(call(body, all_ins, in_specs, shapes, out_specs, scratch, aliases, flops=10 * J * nl * rows * L))
    new = outs.pop(0)
    if last:
        return new, outs[0], outs[1] if write is not None else None
    z = [[outs.pop(0) for _ in z_ports] for _ in z_spans]
    y = [outs.pop(0) for _ in y_ports]
    return new, z, y, outs


def finish(new, own, others, layers, span, anomaly, field, shape):
    J, _, _, L = shape
    k0, kc = span
    nl = len(layers)
    count = len(others) + 1
    buffers = [buffer for buffer in (anomaly, field) if buffer is not None]
    outs_count = 1 if field is None else 2

    def body(*refs):
        u, sums = refs[0], refs[1 : 1 + count]
        outs = refs[1 + count + len(buffers) : 1 + count + len(buffers) + outs_count]
        scaled, sems = refs[-2:]
        copies = []
        if field is not None:
            copies += write_copies(u, outs[1], layers, k0, kc, sems.at[1])
            for copy in copies:
                copy.start()
        results = write_copies(scaled, outs[0], layers, k0, kc, sems.at[0])
        for n in range(nl):

            def tile(t, carry, n=n):
                here = pl.ds(pl.multiple_of(t * ROWS, ROWS), ROWS)
                means = [ref[0, n, here] for ref in sums]
                mean = means[0]
                for other in means[1:]:
                    mean = mean + other
                mean = mean * (1.0 / count)
                spread = None
                for ref, own_mean in zip(sums, means):
                    off = own_mean - mean
                    part = ref[1, n, here] + J * (off * off)
                    spread = part if spread is None else spread + part
                scale = lax.rsqrt(spread * (1.0 / (J * count)) + 0.0001)
                for j in range(J):
                    scaled[j, n, here] = (u[j, n, here] - mean) * scale
                return carry

            lax.fori_loop(0, kc // ROWS, tile, 0)
            results[n].start()
        for copy in copies + results:
            copy.wait()

    ins = [new, own] + list(others)
    aliases = {len(ins) + n: (n if anomaly is not None else 1) for n in range(len(buffers))}
    return call(
        body,
        ins + buffers,
        [VMEM] * len(ins) + [HBM] * len(buffers),
        [jax.ShapeDtypeStruct(shape, F32)] * outs_count,
        [HBM] * outs_count,
        [pltpu.VMEM((J, nl, kc, L), F32), pltpu.SemaphoreType.DMA((2, nl))],
        aliases,
        flops=10 * J * nl * kc * L,
    )


def other_rows(own):
    count = lax.axis_size("rows")
    return [lax.ppermute(own, "rows", [(i, (i + shift) % count) for i in range(count)]) for shift in range(1, count)]


def spans_of(start, extent, weights):
    tiles, total, cuts = extent // ROWS, sum(weights), [0]
    for n in range(1, len(weights) + 1):
        cuts.append(round(tiles * sum(weights[:n]) / total))
    return [(start + a * ROWS, (b - a) * ROWS) for a, b in zip(cuts, cuts[1:]) if b > a]


def on_device(field_values, conductance, source):
    shape = J, I, K, L = field_values.shape
    spans = spans_of(0, K, CHUNKS)
    chunks = range(len(spans))

    def trade(z, y):
        z_got = []
        for faces in z:
            z_got.append(exchange(faces, "cols"))
        return z_got, exchange(y, "rows")

    z_out = cut_faces(field_values, spans[:1], [], False)[0]
    z_rest, y_out, x_out = cut_faces(field_values, spans[1:], spans, True)
    z_out += z_rest
    z_in, y_in = [], []
    for q in chunks:
        z_got, y_got = trade([z_out[q]], y_out[q])
        z_in.append([(*spans[q], z_got[0])])
        y_in.append((y_got, spans[q][0]))
    x_in = exchange(x_out, "slabs")
    staged, conductance, source = stage([field_values, conductance, source])
    fields = [(staged, 0) for _ in chunks]
    for step_no in range(1, STEPS):
        newer, z_next, y_next = [], [], []
        for q in chunks:
            is_end = q == len(spans) - 1
            z_spans = spans_of(*spans[q], LAST_CUT) if is_end and step_no == STEPS - 1 else [spans[q]]
            pieces = [(q, k0, kc, faces) for k0, kc, faces in z_in[q]]
            new, z, y, x_out = step(
                pieces,
                fields,
                conductance,
                source,
                y_in,
                x_in,
                range(I),
                z_spans,
                (newer + [(None, 0)])[0][0] if is_end else None,
                False,
            )
            newer.append((new, spans[q][0]))
            z_got, y_got = trade(z, y)
            z_next.append([(*span, faces) for span, faces in zip(z_spans, z_got)])
            y_next.append((y_got, spans[q][0]))
        x_in = exchange(x_out, "slabs")
        fields, z_in, y_in = newer, z_next, y_next

    inner, outer = list(range(1, I - 1)), [0, I - 1]
    jobs = []
    if inner:
        jobs.append((inner, [(q, *spans[q], []) for q in chunks]))
    for q in chunks:
        for k0, kc, faces in z_in[q]:
            jobs.append((outer, [(q, k0, kc, faces)]))
    anomaly, field, write, sums = None, None, None, []
    for n, (layers, pieces) in enumerate(jobs):
        new, own, wrote = step(pieces, fields, conductance, source, y_in, x_in, layers, [], None, True, write)
        field = field if wrote is None else wrote
        others = other_rows(own)
        span = (pieces[0][1], sum(piece[2] for piece in pieces))
        write = (new, layers, span, field) if n < len(jobs) - 2 else None
        sums.append((new, own, others, layers, span))
    for n, job in enumerate(sums):
        to_field = field if n >= len(sums) - 2 else None
        done = finish(*job, anomaly, to_field, shape)
        anomaly = done[0]
        field = done[1] if to_field is not None else field
    return anomaly, field


def solution(mesh):
    spec = P(("trial", "rows"), "cols", "slabs", None)

    return jax.shard_map(on_device, mesh=mesh, in_specs=(spec, spec, spec), out_specs=(spec, spec), check_vma=False)
```

profile of v0, /device:TPU:0, one launch (start us, length us, event | category | flops | bytes accessed | tf_op | source)
XLA Modules:
  0.0 107.1 jit_solution(11366825781865590699)
XLA Ops:
  1.9 3.1 %collective-permute-start = (f32[16,72,128]{2,1,0:T(8,128)S(1)}, f32[16,72,128]{2,1,0:T(8,128)S(1)}, u32[]{:S(2)}, u32[]{:S(2)}) collective-permute-start(f32[16,72,128]{2,1,0:T(8,128)S(1)} %get-tuple-element.56), channel_id=1, source_target_pairs={{0,4},{4,0},{8,12},{12,8},{1,5},{5,1},{9,13},{13,9},{2,6},{6,2},{1... | collective-permute-start | bytes 1769480 | tf_op jit(solution)/shard_map/ppermute | solution.py:46
  7.0 1.6 %collective-permute-start.2 = (f32[4,72,128]{2,1,0:T(8,128)S(1)}, f32[4,72,128]{2,1,0:T(8,128)S(1)}, u32[]{:S(2)}, u32[]{:S(2)}) collective-permute-start(f32[4,72,128]{2,1,0:T(8,128)S(1)} %get-tuple-element.58), channel_id=1, source_target_pairs={{0,16},{16,0},{1,17},{17,1},{2,18},{18,2},{3,19},{19,3},{4,20},{20... | collective-permute-start | bytes 442376 | tf_op jit(solution)/shard_map/ppermute | solution.py:46
  10.1 4.4 %collective-permute-start.4 = (f32[16,56,128]{2,1,0:T(8,128)S(1)}, f32[16,56,128]{2,1,0:T(8,128)S(1)}, u32[]{:S(2)}, u32[]{:S(2)}) collective-permute-start(f32[16,56,128]{2,1,0:T(8,128)S(1)} %get-tuple-element.61), channel_id=1, source_target_pairs={{0,4},{4,0},{8,12},{12,8},{1,5},{5,1},{9,13},{13,9},{2,6},{6,2},{1... | collective-permute-start | bytes 1376264 | tf_op jit(solution)/shard_map/ppermute | solution.py:46
  14.5 4.7 %shard_map.50 = (f32[16,4,128,128]{3,2,1,0:T(8,128)S(1)}, f32[16,4,128,128]{3,2,1,0:T(8,128)S(1)}, f32[16,4,128,128]{3,2,1,0:T(8,128)S(1)}) custom-call(f32[16,4,128,128]{3,2,1,0:T(8,128)} %u.3, f32[16,4,128,128]{3,2,1,0:T(8,128)} %refs_1_.1, f32[16,4,128,128]{3,2,1,0:T(8,128)} %refs_2_.1), custom_call_target="tpu_custom_call" | custom-call | tf_op jit(solution)/shard_map/pallas_call | solution.py:23
  19.9 1.6 %shard_map.53 = (f32[16,4,72,128]{3,2,1,0:T(8,128)S(1)}, f32[16,72,128]{2,1,0:T(8,128)S(1)}, f32[16,72,128]{2,1,0:T(8,128)S(1)}, f32[4,72,128]{2,1,0:T(8,128)S(1)}) custom-call(f32[16,4,128,128]{3,2,1,0:T(8,128)S(1)} %get-tuple-element.53.refs_0_, f32[16,4,128,128]{3,2,1,0:T(8,128)S(1)} %get-tuple-element.54.refs_1_, ...), custom_call_target="tpu_custom_call" | custom-call | flops 5898240 | tf_op jit(solution)/shard_map/pallas_call | solution.py:23
  21.5 4.1 %collective-permute-start.7 = (f32[16,72,128]{2,1,0:T(8,128)S(1)}, f32[16,72,128]{2,1,0:T(8,128)S(1)}, u32[]{:S(2)}, u32[]{:S(2)}) collective-permute-start(f32[16,72,128]{2,1,0:T(8,128)S(1)} %get-tuple-element.65), channel_id=1, source_target_pairs={{0,4},{4,0},{8,12},{12,8},{1,5},{5,1},{9,13},{13,9},{2,6},{6,2},{1... | collective-permute-start | bytes 1769480 | tf_op jit(solution)/shard_map/ppermute | solution.py:46
  26.3 1.9 %collective-permute-start.6 = (f32[4,56,128]{2,1,0:T(8,128)S(1)}, f32[4,56,128]{2,1,0:T(8,128)S(1)}, u32[]{:S(2)}, u32[]{:S(2)}) collective-permute-start(f32[4,56,128]{2,1,0:T(8,128)S(1)} %get-tuple-element.63), channel_id=1, source_target_pairs={{0,16},{16,0},{1,17},{17,1},{2,18},{18,2},{3,19},{19,3},{4,20},{20... | collective-permute-start | bytes 344072 | tf_op jit(solution)/shard_map/ppermute | solution.py:46
  28.2 3.2 %collective-permute-done.6.refs_5_ = f32[4,56,128]{2,1,0:T(8,128)S(1)} collective-permute-done((f32[4,56,128]{2,1,0:T(8,128)S(1)}, f32[4,56,128]{2,1,0:T(8,128)S(1)}, u32[]{:S(2)}, u32[]{:S(2)}) %collective-permute-start.6) | collective-permute-done | bytes 114720 | tf_op jit(solution)/shard_map/ppermute | solution.py:46
  31.4 2.2 %collective-permute-start.9 = (f32[4,72,128]{2,1,0:T(8,128)S(1)}, f32[4,72,128]{2,1,0:T(8,128)S(1)}, u32[]{:S(2)}, u32[]{:S(2)}) collective-permute-start(f32[4,72,128]{2,1,0:T(8,128)S(1)} %get-tuple-element.67), channel_id=1, source_target_pairs={{0,16},{16,0},{1,17},{17,1},{2,18},{18,2},{3,19},{19,3},{4,20},{20... | collective-permute-start | bytes 442376 | tf_op jit(solution)/shard_map/ppermute | solution.py:46
  35.0 1.6 %collective-permute-start.10 = (f32[16,4,128]{2,1,0:T(4,128)S(1)}, f32[16,4,128]{2,1,0:T(4,128)S(1)}, u32[]{:S(2)}, u32[]{:S(2)}) collective-permute-start(f32[16,4,128]{2,1,0:T(4,128)S(1)} %get-tuple-element.68), channel_id=1, source_target_pairs={{0,2},{2,0},{1,3},{3,1},{4,6},{6,4},{5,7},{7,5},{8,10},{10,8},{9,1... | collective-permute-start | bytes 98312 | tf_op jit(solution)/shard_map/ppermute | solution.py:46
  36.6 3.8 %collective-permute-start.11 = (f32[16,56,128]{2,1,0:T(8,128)S(1)}, f32[16,56,128]{2,1,0:T(8,128)S(1)}, u32[]{:S(2)}, u32[]{:S(2)}) collective-permute-start(f32[16,56,128]{2,1,0:T(8,128)S(1)} %get-tuple-element.70), channel_id=1, source_target_pairs={{0,4},{4,0},{8,12},{12,8},{1,5},{5,1},{9,13},{13,9},{2,6},{6,2},{1... | collective-permute-start | bytes 1376264 | tf_op jit(solution)/shard_map/ppermute | solution.py:46
  42.7 5.5 %collective-permute-start.14 = (f32[16,72,128]{2,1,0:T(8,128)S(1)}, f32[16,72,128]{2,1,0:T(8,128)S(1)}, u32[]{:S(2)}, u32[]{:S(2)}) collective-permute-start(f32[16,72,128]{2,1,0:T(8,128)S(1)} %get-tuple-element.74), channel_id=1, source_target_pairs={{0,4},{4,0},{8,12},{12,8},{1,5},{5,1},{9,13},{13,9},{2,6},{6,2},{1... | collective-permute-start | bytes 1769480 | tf_op jit(solution)/shard_map/ppermute | solution.py:46
  50.1 3.6 %collective-permute-done.13.refs_6_ = f32[4,56,128]{2,1,0:T(8,128)S(1)} collective-permute-done((f32[4,56,128]{2,1,0:T(8,128)S(1)}, f32[4,56,128]{2,1,0:T(8,128)S(1)}, u32[]{:S(2)}, u32[]{:S(2)}) %collective-permute-start.13) | collective-permute-done | bytes 114720 | tf_op jit(solution)/shard_map/ppermute | solution.py:46
  54.7 4.4 %collective-permute-start.18 = (f32[16,56,128]{2,1,0:T(8,128)S(1)}, f32[16,56,128]{2,1,0:T(8,128)S(1)}, u32[]{:S(2)}, u32[]{:S(2)}) collective-permute-start(f32[16,56,128]{2,1,0:T(8,128)S(1)} %get-tuple-element.79), channel_id=1, source_target_pairs={{0,4},{4,0},{8,12},{12,8},{1,5},{5,1},{9,13},{13,9},{2,6},{6,2},{1... | collective-permute-start | bytes 1376264 | tf_op jit(solution)/shard_map/ppermute | solution.py:46
  59.8 1.6 %collective-permute-start.17 = (f32[16,4,128]{2,1,0:T(4,128)S(1)}, f32[16,4,128]{2,1,0:T(4,128)S(1)}, u32[]{:S(2)}, u32[]{:S(2)}) collective-permute-start(f32[16,4,128]{2,1,0:T(4,128)S(1)} %get-tuple-element.77), channel_id=1, source_target_pairs={{0,2},{2,0},{1,3},{3,1},{4,6},{6,4},{5,7},{7,5},{8,10},{10,8},{9,1... | collective-permute-start | bytes 98312 | tf_op jit(solution)/shard_map/ppermute | solution.py:46
  61.3 2.4 %collective-permute-done.17.refs_7_ = f32[16,4,128]{2,1,0:T(4,128)S(1)} collective-permute-done((f32[16,4,128]{2,1,0:T(4,128)S(1)}, f32[16,4,128]{2,1,0:T(4,128)S(1)}, u32[]{:S(2)}, u32[]{:S(2)}) %collective-permute-start.17) | collective-permute-done | bytes 32800 | tf_op jit(solution)/shard_map/ppermute | solution.py:46
  64.3 4.6 %collective-permute-done.16.refs_6_ = f32[4,72,128]{2,1,0:T(8,128)S(1)} collective-permute-done((f32[4,72,128]{2,1,0:T(8,128)S(1)}, f32[4,72,128]{2,1,0:T(8,128)S(1)}, u32[]{:S(2)}, u32[]{:S(2)}) %collective-permute-start.16) | collective-permute-done | bytes 147488 | tf_op jit(solution)/shard_map/ppermute | solution.py:46
  70.0 1.9 %collective-permute-start.28 = (f32[16,72,128]{2,1,0:T(8,128)S(1)}, f32[16,72,128]{2,1,0:T(8,128)S(1)}, u32[]{:S(2)}, u32[]{:S(2)}) collective-permute-start(f32[16,72,128]{2,1,0:T(8,128)S(1)} %get-tuple-element.91), channel_id=1, source_target_pairs={{0,4},{4,0},{8,12},{12,8},{1,5},{5,1},{9,13},{13,9},{2,6},{6,2},{1... | collective-permute-start | bytes 1769480 | tf_op jit(solution)/shard_map/ppermute | solution.py:46
  74.1 4.2 %collective-permute-done.20.refs_6_ = f32[4,56,128]{2,1,0:T(8,128)S(1)} collective-permute-done((f32[4,56,128]{2,1,0:T(8,128)S(1)}, f32[4,56,128]{2,1,0:T(8,128)S(1)}, u32[]{:S(2)}, u32[]{:S(2)}) %collective-permute-start.20) | collective-permute-done | bytes 114720 | tf_op jit(solution)/shard_map/ppermute | solution.py:46
  79.2 1.7 %collective-permute-start.23 = (f32[4,56,128]{2,1,0:T(8,128)S(1)}, f32[4,56,128]{2,1,0:T(8,128)S(1)}, u32[]{:S(2)}, u32[]{:S(2)}) collective-permute-start(f32[4,56,128]{2,1,0:T(8,128)S(1)} %get-tuple-element.85), channel_id=1, source_target_pairs={{0,16},{16,0},{1,17},{17,1},{2,18},{18,2},{3,19},{19,3},{4,20},{20... | collective-permute-start | bytes 344072 | tf_op jit(solution)/shard_map/ppermute | solution.py:46
  83.5 2.4 %collective-permute-done.24.refs_7_.refs_6_ = f32[16,4,128]{2,1,0:T(4,128)S(1)} collective-permute-done((f32[16,4,128]{2,1,0:T(4,128)S(1)}, f32[16,4,128]{2,1,0:T(4,128)S(1)}, u32[]{:S(2)}, u32[]{:S(2)}) %collective-permute-start.24) | collective-permute-done | bytes 32800 | tf_op jit(solution)/shard_map/ppermute | solution.py:46
  88.2 4.3 %collective-permute-done.30.refs_4_.refs_6_ = f32[4,72,128]{2,1,0:T(8,128)S(1)} collective-permute-done((f32[4,72,128]{2,1,0:T(8,128)S(1)}, f32[4,72,128]{2,1,0:T(8,128)S(1)}, u32[]{:S(2)}, u32[]{:S(2)}) %collective-permute-start.30) | collective-permute-done | bytes 147488 | tf_op jit(solution)/shard_map/ppermute | solution.py:46
  93.8 1.6 %collective-permute-start.33 = (f32[2,2,128,128]{3,2,1,0:T(8,128)S(1)}, f32[2,2,128,128]{3,2,1,0:T(8,128)S(1)}, u32[]{:S(2)}, u32[]{:S(2)}) collective-permute-start(f32[2,2,128,128]{3,2,1,0:T(8,128)S(1)} %get-tuple-element.100.refs_1_), channel_id=1, source_target_pairs={{0,16},{16,0},{1,17},{17,1},{2,18},{18,2},{3,19},{19,3},{4,20},{20... | collective-permute-start | bytes 786440 | tf_op jit(solution)/shard_map/ppermute | solution.py:361
  102.1 1.8 %shard_map.63.refs_3_ = f32[16,4,128,128]{3,2,1,0:T(8,128)} custom-call(f32[16,2,128,128]{3,2,1,0:T(8,128)S(1)} %get-tuple-element.94.refs_8_.refs_0_, f32[2,2,128,128]{3,2,1,0:T(8,128)S(1)} %get-tuple-element.100.refs_1_, f32[2,2,128,128]{3,2,1,0:T(8,128)S(1)} %collective-permute-done.33.refs_2_), custom_call_target="tpu_custom_call" | custom-call | flops 5242880 | tf_op jit(solution)/shard_map/pallas_call | solution.py:23
  (61 shorter events, 34.2 us)
Async XLA Ops:
  1.9 18.0 %collective-permute-start = (f32[16,72,128]{2,1,0:T(8,128)S(1)}, f32[16,72,128]{2,1,0:T(8,128)S(1)}, u32[]{:S(2)}, u32[]{:S(2)}) collective-permute-start(f32[16,72,128]{2,1,0:T(8,128)S(1)} %get-tuple-element.56), channel_id=1, source_target_pairs={{0,4},{4,0},{8,12},{12,8},{1,5},{5,1},{9,13},{13,9},{2,6},{6,2},{1... | collective-permute-start | bytes 1769480 | tf_op jit(solution)/shard_map/ppermute | solution.py:46
  5.0 14.9 %collective-permute-start.1 = (f32[16,72,128]{2,1,0:T(8,128)S(1)}, f32[16,72,128]{2,1,0:T(8,128)S(1)}, u32[]{:S(2)}, u32[]{:S(2)}) collective-permute-start(f32[16,72,128]{2,1,0:T(8,128)S(1)} %get-tuple-element.57), channel_id=1, source_target_pairs={{4,8},{8,4},{5,9},{9,5},{6,10},{10,6},{7,11},{11,7},{20,24},{24,20... | collective-permute-start | bytes 1769480 | tf_op jit(solution)/shard_map/ppermute | solution.py:46
  7.0 12.8 %collective-permute-start.2 = (f32[4,72,128]{2,1,0:T(8,128)S(1)}, f32[4,72,128]{2,1,0:T(8,128)S(1)}, u32[]{:S(2)}, u32[]{:S(2)}) collective-permute-start(f32[4,72,128]{2,1,0:T(8,128)S(1)} %get-tuple-element.58), channel_id=1, source_target_pairs={{0,16},{16,0},{1,17},{17,1},{2,18},{18,2},{3,19},{19,3},{4,20},{20... | collective-permute-start | bytes 442376 | tf_op jit(solution)/shard_map/ppermute | solution.py:46
  8.6 10.5 %collective-permute-start.3 = (f32[16,4,128]{2,1,0:T(4,128)S(1)}, f32[16,4,128]{2,1,0:T(4,128)S(1)}, u32[]{:S(2)}, u32[]{:S(2)}) collective-permute-start(f32[16,4,128]{2,1,0:T(4,128)S(1)} %get-tuple-element.59), channel_id=1, source_target_pairs={{0,2},{2,0},{1,3},{3,1},{4,6},{6,4},{5,7},{7,5},{8,10},{10,8},{9,1... | collective-permute-start | bytes 98312 | tf_op jit(solution)/shard_map/ppermute | solution.py:46
  10.1 23.6 %collective-permute-start.4 = (f32[16,56,128]{2,1,0:T(8,128)S(1)}, f32[16,56,128]{2,1,0:T(8,128)S(1)}, u32[]{:S(2)}, u32[]{:S(2)}) collective-permute-start(f32[16,56,128]{2,1,0:T(8,128)S(1)} %get-tuple-element.61), channel_id=1, source_target_pairs={{0,4},{4,0},{8,12},{12,8},{1,5},{5,1},{9,13},{13,9},{2,6},{6,2},{1... | collective-permute-start | bytes 1376264 | tf_op jit(solution)/shard_map/ppermute | solution.py:46
  19.2 14.5 %collective-permute-start.5 = (f32[16,56,128]{2,1,0:T(8,128)S(1)}, f32[16,56,128]{2,1,0:T(8,128)S(1)}, u32[]{:S(2)}, u32[]{:S(2)}) collective-permute-start(f32[16,56,128]{2,1,0:T(8,128)S(1)} %get-tuple-element.62), channel_id=1, source_target_pairs={{4,8},{8,4},{5,9},{9,5},{6,10},{10,6},{7,11},{11,7},{20,24},{24,20... | collective-permute-start | bytes 1376264 | tf_op jit(solution)/shard_map/ppermute | solution.py:46
  21.5 20.2 %collective-permute-start.7 = (f32[16,72,128]{2,1,0:T(8,128)S(1)}, f32[16,72,128]{2,1,0:T(8,128)S(1)}, u32[]{:S(2)}, u32[]{:S(2)}) collective-permute-start(f32[16,72,128]{2,1,0:T(8,128)S(1)} %get-tuple-element.65), channel_id=1, source_target_pairs={{0,4},{4,0},{8,12},{12,8},{1,5},{5,1},{9,13},{13,9},{2,6},{6,2},{1... | collective-permute-start | bytes 1769480 | tf_op jit(solution)/shard_map/ppermute | solution.py:46
  25.6 16.1 %collective-permute-start.8 = (f32[16,72,128]{2,1,0:T(8,128)S(1)}, f32[16,72,128]{2,1,0:T(8,128)S(1)}, u32[]{:S(2)}, u32[]{:S(2)}) collective-permute-start(f32[16,72,128]{2,1,0:T(8,128)S(1)} %get-tuple-element.66), channel_id=1, source_target_pairs={{4,8},{8,4},{5,9},{9,5},{6,10},{10,6},{7,11},{11,7},{20,24},{24,20... | collective-permute-start | bytes 1769480 | tf_op jit(solution)/shard_map/ppermute | solution.py:46
  31.4 9.6 %collective-permute-start.9 = (f32[4,72,128]{2,1,0:T(8,128)S(1)}, f32[4,72,128]{2,1,0:T(8,128)S(1)}, u32[]{:S(2)}, u32[]{:S(2)}) collective-permute-start(f32[4,72,128]{2,1,0:T(8,128)S(1)} %get-tuple-element.67), channel_id=1, source_target_pairs={{0,16},{16,0},{1,17},{17,1},{2,18},{18,2},{3,19},{19,3},{4,20},{20... | collective-permute-start | bytes 442376 | tf_op jit(solution)/shard_map/ppermute | solution.py:46
  36.6 17.2 %collective-permute-start.11 = (f32[16,56,128]{2,1,0:T(8,128)S(1)}, f32[16,56,128]{2,1,0:T(8,128)S(1)}, u32[]{:S(2)}, u32[]{:S(2)}) collective-permute-start(f32[16,56,128]{2,1,0:T(8,128)S(1)} %get-tuple-element.70), channel_id=1, source_target_pairs={{0,4},{4,0},{8,12},{12,8},{1,5},{5,1},{9,13},{13,9},{2,6},{6,2},{1... | collective-permute-start | bytes 1376264 | tf_op jit(solution)/shard_map/ppermute | solution.py:46
  40.4 13.4 %collective-permute-start.12 = (f32[16,56,128]{2,1,0:T(8,128)S(1)}, f32[16,56,128]{2,1,0:T(8,128)S(1)}, u32[]{:S(2)}, u32[]{:S(2)}) collective-permute-start(f32[16,56,128]{2,1,0:T(8,128)S(1)} %get-tuple-element.71), channel_id=1, source_target_pairs={{4,8},{8,4},{5,9},{9,5},{6,10},{10,6},{7,11},{11,7},{20,24},{24,20... | collective-permute-start | bytes 1376264 | tf_op jit(solution)/shard_map/ppermute | solution.py:46
  42.7 26.2 %collective-permute-start.14 = (f32[16,72,128]{2,1,0:T(8,128)S(1)}, f32[16,72,128]{2,1,0:T(8,128)S(1)}, u32[]{:S(2)}, u32[]{:S(2)}) collective-permute-start(f32[16,72,128]{2,1,0:T(8,128)S(1)} %get-tuple-element.74), channel_id=1, source_target_pairs={{0,4},{4,0},{8,12},{12,8},{1,5},{5,1},{9,13},{13,9},{2,6},{6,2},{1... | collective-permute-start | bytes 1769480 | tf_op jit(solution)/shard_map/ppermute | solution.py:46
  48.2 20.7 %collective-permute-start.15 = (f32[16,72,128]{2,1,0:T(8,128)S(1)}, f32[16,72,128]{2,1,0:T(8,128)S(1)}, u32[]{:S(2)}, u32[]{:S(2)}) collective-permute-start(f32[16,72,128]{2,1,0:T(8,128)S(1)} %get-tuple-element.75), channel_id=1, source_target_pairs={{4,8},{8,4},{5,9},{9,5},{6,10},{10,6},{7,11},{11,7},{20,24},{24,20... | collective-permute-start | bytes 1769480 | tf_op jit(solution)/shard_map/ppermute | solution.py:46
  54.7 23.5 %collective-permute-start.18 = (f32[16,56,128]{2,1,0:T(8,128)S(1)}, f32[16,56,128]{2,1,0:T(8,128)S(1)}, u32[]{:S(2)}, u32[]{:S(2)}) collective-permute-start(f32[16,56,128]{2,1,0:T(8,128)S(1)} %get-tuple-element.79), channel_id=1, source_target_pairs={{0,4},{4,0},{8,12},{12,8},{1,5},{5,1},{9,13},{13,9},{2,6},{6,2},{1... | collective-permute-start | bytes 1376264 | tf_op jit(solution)/shard_map/ppermute | solution.py:46
  59.1 19.1 %collective-permute-start.19 = (f32[16,56,128]{2,1,0:T(8,128)S(1)}, f32[16,56,128]{2,1,0:T(8,128)S(1)}, u32[]{:S(2)}, u32[]{:S(2)}) collective-permute-start(f32[16,56,128]{2,1,0:T(8,128)S(1)} %get-tuple-element.80), channel_id=1, source_target_pairs={{4,8},{8,4},{5,9},{9,5},{6,10},{10,6},{7,11},{11,7},{20,24},{24,20... | collective-permute-start | bytes 1376264 | tf_op jit(solution)/shard_map/ppermute | solution.py:46
  70.0 25.4 %collective-permute-start.28 = (f32[16,72,128]{2,1,0:T(8,128)S(1)}, f32[16,72,128]{2,1,0:T(8,128)S(1)}, u32[]{:S(2)}, u32[]{:S(2)}) collective-permute-start(f32[16,72,128]{2,1,0:T(8,128)S(1)} %get-tuple-element.91), channel_id=1, source_target_pairs={{0,4},{4,0},{8,12},{12,8},{1,5},{5,1},{9,13},{13,9},{2,6},{6,2},{1... | collective-permute-start | bytes 1769480 | tf_op jit(solution)/shard_map/ppermute | solution.py:46
  71.8 23.8 %collective-permute-start.29 = (f32[16,72,128]{2,1,0:T(8,128)S(1)}, f32[16,72,128]{2,1,0:T(8,128)S(1)}, u32[]{:S(2)}, u32[]{:S(2)}) collective-permute-start(f32[16,72,128]{2,1,0:T(8,128)S(1)} %get-tuple-element.92), channel_id=1, source_target_pairs={{4,8},{8,4},{5,9},{9,5},{6,10},{10,6},{7,11},{11,7},{20,24},{24,20... | collective-permute-start | bytes 1769480 | tf_op jit(solution)/shard_map/ppermute | solution.py:46
  72.5 5.7 %collective-permute-start.20 = (f32[4,56,128]{2,1,0:T(8,128)S(1)}, f32[4,56,128]{2,1,0:T(8,128)S(1)}, u32[]{:S(2)}, u32[]{:S(2)}) collective-permute-start(f32[4,56,128]{2,1,0:T(8,128)S(1)} %get-tuple-element.81), channel_id=1, source_target_pairs={{0,16},{16,0},{1,17},{17,1},{2,18},{18,2},{3,19},{19,3},{4,20},{20... | collective-permute-start | bytes 344072 | tf_op jit(solution)/shard_map/ppermute | solution.py:46
  79.2 8.3 %collective-permute-start.23 = (f32[4,56,128]{2,1,0:T(8,128)S(1)}, f32[4,56,128]{2,1,0:T(8,128)S(1)}, u32[]{:S(2)}, u32[]{:S(2)}) collective-permute-start(f32[4,56,128]{2,1,0:T(8,128)S(1)} %get-tuple-element.85), channel_id=1, source_target_pairs={{0,16},{16,0},{1,17},{17,1},{2,18},{18,2},{3,19},{19,3},{4,20},{20... | collective-permute-start | bytes 344072 | tf_op jit(solution)/shard_map/ppermute | solution.py:46
  80.9 16.8 %collective-permute-start.26 = (f32[16,40,128]{2,1,0:T(8,128)S(1)}, f32[16,40,128]{2,1,0:T(8,128)S(1)}, u32[]{:S(2)}, u32[]{:S(2)}) collective-permute-start(f32[16,40,128]{2,1,0:T(8,128)S(1)} %get-tuple-element.89), channel_id=1, source_target_pairs={{0,4},{4,0},{8,12},{12,8},{1,5},{5,1},{9,13},{13,9},{2,6},{6,2},{1... | collective-permute-start | bytes 983048 | tf_op jit(solution)/shard_map/ppermute | solution.py:46
  86.0 6.5 %collective-permute-start.30 = (f32[4,72,128]{2,1,0:T(8,128)S(1)}, f32[4,72,128]{2,1,0:T(8,128)S(1)}, u32[]{:S(2)}, u32[]{:S(2)}) collective-permute-start(f32[4,72,128]{2,1,0:T(8,128)S(1)} %get-tuple-element.93), channel_id=1, source_target_pairs={{0,16},{16,0},{1,17},{17,1},{2,18},{18,2},{3,19},{19,3},{4,20},{20... | collective-permute-start | bytes 442376 | tf_op jit(solution)/shard_map/ppermute | solution.py:46
  87.5 11.3 %collective-permute-start.27 = (f32[16,40,128]{2,1,0:T(8,128)S(1)}, f32[16,40,128]{2,1,0:T(8,128)S(1)}, u32[]{:S(2)}, u32[]{:S(2)}) collective-permute-start(f32[16,40,128]{2,1,0:T(8,128)S(1)} %get-tuple-element.90), channel_id=1, source_target_pairs={{4,8},{8,4},{5,9},{9,5},{6,10},{10,6},{7,11},{11,7},{20,24},{24,20... | collective-permute-start | bytes 983048 | tf_op jit(solution)/shard_map/ppermute | solution.py:46
  93.8 8.3 %collective-permute-start.33 = (f32[2,2,128,128]{3,2,1,0:T(8,128)S(1)}, f32[2,2,128,128]{3,2,1,0:T(8,128)S(1)}, u32[]{:S(2)}, u32[]{:S(2)}) collective-permute-start(f32[2,2,128,128]{3,2,1,0:T(8,128)S(1)} %get-tuple-element.100.refs_1_), channel_id=1, source_target_pairs={{0,16},{16,0},{1,17},{17,1},{2,18},{18,2},{3,19},{19,3},{4,20},{20... | collective-permute-start | bytes 786440 | tf_op jit(solution)/shard_map/ppermute | solution.py:361
  97.7 6.3 %collective-permute-start.32 = (f32[2,2,72,128]{3,2,1,0:T(8,128)S(1)}, f32[2,2,72,128]{3,2,1,0:T(8,128)S(1)}, u32[]{:S(2)}, u32[]{:S(2)}) collective-permute-start(f32[2,2,72,128]{3,2,1,0:T(8,128)S(1)} %get-tuple-element.99.refs_1_), channel_id=1, source_target_pairs={{0,16},{16,0},{1,17},{17,1},{2,18},{18,2},{3,19},{19,3},{4,20},{20... | collective-permute-start | bytes 442376 | tf_op jit(solution)/shard_map/ppermute | solution.py:361
  (10 other events, 49.7 us)
where the time goes:
time: 108 us; the launch traced here: 107 us
  starting transfers between devices  57.7 us (53%)
  waiting for transfers between devices  25.5 us (24%)
  Pallas kernels  23 us (21%)
    ppermute x30, starting transfers between devices, exchange(): received.append(lax.ppermute(buffer, axis, perm))  52.9 us
    ppermute x30, waiting for transfers between devices, exchange(): received.append(lax.ppermute(buffer, axis, perm))  25.5 us
    pallas_call x17, Pallas kernels, call(): pl.pallas_call(body, in_specs=in_specs, out_shape=outs, out_specs=out_spe...  23 us
    ppermute x4, starting transfers between devices, other_rows(): lax.ppermute(own, 'rows', [(i, (i + shift) % count) for i in range(count)])  4.82 us
  transfers between devices with their start and end apart: 34, of which 8 were waited for; matrix products, arithmetic and copies ran while one was open for 0% of the time, Pallas kernels for 20%

commit v1 on v0

--- a/solution.py
+++ b/solution.py
@@ -37,13 +37,15 @@
 
 
 def exchange(buffers, axis):
-    count = lax.axis_size(axis)
+    count, trials = lax.axis_size(axis), lax.axis_size("trial")
     received = []
     for port, buffer in zip(ports_of(axis), buffers):
-        perm = []
+        pairs, alone = [], set(range(count))
         for i in range(port, count - 1, 2):
-            perm += [(i, i + 1), (i + 1, i)]
-        received.append(lax.ppermute(buffer, axis, perm))
+            pairs += [(i * trials + t, (i + 1) * trials + t) for t in range(trials)]
+            alone -= {i, i + 1}
+        pairs += [(i * trials + t, i * trials + t + 1) for i in sorted(alone) for t in range(0, trials - 1, 2)]
+        received.append(lax.ppermute(buffer, (axis, "trial"), pairs + [(b, a) for a, b in pairs]))
     return received
 
 
@@ -57,14 +59,14 @@
 
 
 def halo_readers(axis, refs):
-    upper = is_upper(axis, 0)
+    at, upper = lax.axis_index(axis), is_upper(axis, 0)
+    has_lower = (at > 0).astype(F32)
+    has_upper = (at < lax.axis_size(axis) - 1).astype(F32)
     if len(refs) == 1:
-        has_lower = upper.astype(F32)
-        has_upper = (1 - upper).astype(F32)
         return (lambda where: refs[0][where] * has_lower), (lambda where: refs[0][where] * has_upper)
     return (
-        lambda where: jnp.where(upper == 1, refs[0][where], refs[1][where]),
-        lambda where: jnp.where(upper == 1, refs[1][where], refs[0][where]),
+        lambda where: jnp.where(upper == 1, refs[0][where], refs[1][where]) * has_lower,
+        lambda where: jnp.where(upper == 1, refs[1][where], refs[0][where]) * has_upper,
     )
 
 

time: 108 us -> 104 us (0.963); the launches traced: 107 us -> 104 us
  starting transfers between devices: 57.7 us -> 45.7 us
  waiting for transfers between devices: 25.5 us -> 34.6 us
    ppermute x30, starting transfers between devices: 52.9 us -> 41.1 us  [exchange(): lax.ppermute(buffer, (axis, 'trial'), pairs + [(b, a) for a, b in pairs])]
    ppermute x30, waiting for transfers between devices: 25.5 us -> 34.3 us  [exchange(): lax.ppermute(buffer, (axis, 'trial'), pairs + [(b, a) for a, b in pairs])]
  transfers between devices with their start and end apart: 34 -> 34, of which waited for: 8 -> 11; matrix products, arithmetic and copies ran while one was open for 0% -> 0% of each run, Pallas kernels for 20% -> 20%
where the time goes in v1:
time: 104 us
  starting transfers between devices  45.7 us (44%)
  waiting for transfers between devices  34.6 us (33%)
  Pallas kernels  23.1 us (22%)
    ppermute x30, starting transfers between devices, exchange(): lax.ppermute(buffer, (axis, 'trial'), pairs + [(b, a) for a, b in pairs])  41.1 us
    ppermute x30, waiting for transfers between devices, exchange(): lax.ppermute(buffer, (axis, 'trial'), pairs + [(b, a) for a, b in pairs])  34.3 us
    pallas_call x17, Pallas kernels, call(): pl.pallas_call(body, in_specs=in_specs, out_shape=outs, out_specs=out_spe...  23.1 us
    ppermute x4, starting transfers between devices, other_rows(): lax.ppermute(own, 'rows', [(i, (i + shift) % count) for i in range(count)])  4.6 us
  transfers between devices with their start and end apart: 34, of which 11 were waited for; matrix products, arithmetic and copies ran while one was open for 0% of the time, Pallas kernels for 20%

profile of v1, /device:TPU:0, one launch (start us, length us, event | category | flops | bytes accessed | tf_op | source)
XLA Modules:
  0.0 104.2 jit_solution(6741165414275013073)
XLA Ops:
  1.9 3.1 %collective-permute-start = (f32[16,72,128]{2,1,0:T(8,128)S(1)}, f32[16,72,128]{2,1,0:T(8,128)S(1)}, u32[]{:S(2)}, u32[]{:S(2)}) collective-permute-start(f32[16,72,128]{2,1,0:T(8,128)S(1)} %get-tuple-element.56), channel_id=1, source_target_pairs={{0,4},{1,5},{8,12},{9,13},{4,0},{5,1},{12,8},{13,9},{2,6},{3,7},{1... | collective-permute-start | bytes 1769480 | tf_op jit(solution)/shard_map/ppermute | solution.py:48
  6.3 1.6 %collective-permute-start.2 = (f32[4,72,128]{2,1,0:T(8,128)S(1)}, f32[4,72,128]{2,1,0:T(8,128)S(1)}, u32[]{:S(2)}, u32[]{:S(2)}) collective-permute-start(f32[4,72,128]{2,1,0:T(8,128)S(1)} %get-tuple-element.58), channel_id=1, source_target_pairs={{0,16},{1,17},{16,0},{17,1},{2,18},{3,19},{18,2},{19,3},{4,20},{5,... | collective-permute-start | bytes 442376 | tf_op jit(solution)/shard_map/ppermute | solution.py:48
  9.4 3.1 %collective-permute-start.4 = (f32[16,56,128]{2,1,0:T(8,128)S(1)}, f32[16,56,128]{2,1,0:T(8,128)S(1)}, u32[]{:S(2)}, u32[]{:S(2)}) collective-permute-start(f32[16,56,128]{2,1,0:T(8,128)S(1)} %get-tuple-element.61), channel_id=1, source_target_pairs={{0,4},{1,5},{8,12},{9,13},{4,0},{5,1},{12,8},{13,9},{2,6},{3,7},{1... | collective-permute-start | bytes 1376264 | tf_op jit(solution)/shard_map/ppermute | solution.py:48
  12.5 4.7 %shard_map.50 = (f32[16,4,128,128]{3,2,1,0:T(8,128)S(1)}, f32[16,4,128,128]{3,2,1,0:T(8,128)S(1)}, f32[16,4,128,128]{3,2,1,0:T(8,128)S(1)}) custom-call(f32[16,4,128,128]{3,2,1,0:T(8,128)} %u.3, f32[16,4,128,128]{3,2,1,0:T(8,128)} %refs_1_.1, f32[16,4,128,128]{3,2,1,0:T(8,128)} %refs_2_.1), custom_call_target="tpu_custom_call" | custom-call | tf_op jit(solution)/shard_map/pallas_call | solution.py:23
  17.3 1.9 %collective-permute-done.refs_3_ = f32[16,72,128]{2,1,0:T(8,128)S(1)} collective-permute-done((f32[16,72,128]{2,1,0:T(8,128)S(1)}, f32[16,72,128]{2,1,0:T(8,128)S(1)}, u32[]{:S(2)}, u32[]{:S(2)}) %collective-permute-start) | collective-permute-done | bytes 589856 | tf_op jit(solution)/shard_map/ppermute | solution.py:48
  19.2 1.6 %shard_map.53 = (f32[16,4,72,128]{3,2,1,0:T(8,128)S(1)}, f32[16,72,128]{2,1,0:T(8,128)S(1)}, f32[16,72,128]{2,1,0:T(8,128)S(1)}, f32[4,72,128]{2,1,0:T(8,128)S(1)}) custom-call(f32[16,4,128,128]{3,2,1,0:T(8,128)S(1)} %get-tuple-element.53.refs_0_, f32[16,4,128,128]{3,2,1,0:T(8,128)S(1)} %get-tuple-element.54.refs_1_, ...), custom_call_target="tpu_custom_call" | custom-call | flops 5898240 | tf_op jit(solution)/shard_map/pallas_call | solution.py:23
  20.8 3.2 %collective-permute-start.7 = (f32[16,72,128]{2,1,0:T(8,128)S(1)}, f32[16,72,128]{2,1,0:T(8,128)S(1)}, u32[]{:S(2)}, u32[]{:S(2)}) collective-permute-start(f32[16,72,128]{2,1,0:T(8,128)S(1)} %get-tuple-element.65), channel_id=1, source_target_pairs={{0,4},{1,5},{8,12},{9,13},{4,0},{5,1},{12,8},{13,9},{2,6},{3,7},{1... | collective-permute-start | bytes 1769480 | tf_op jit(solution)/shard_map/ppermute | solution.py:48
  25.6 4.0 %collective-permute-done.6.refs_5_ = f32[4,56,128]{2,1,0:T(8,128)S(1)} collective-permute-done((f32[4,56,128]{2,1,0:T(8,128)S(1)}, f32[4,56,128]{2,1,0:T(8,128)S(1)}, u32[]{:S(2)}, u32[]{:S(2)}) %collective-permute-start.6) | collective-permute-done | bytes 114720 | tf_op jit(solution)/shard_map/ppermute | solution.py:48
  34.0 2.4 %collective-permute-start.11 = (f32[16,56,128]{2,1,0:T(8,128)S(1)}, f32[16,56,128]{2,1,0:T(8,128)S(1)}, u32[]{:S(2)}, u32[]{:S(2)}) collective-permute-start(f32[16,56,128]{2,1,0:T(8,128)S(1)} %get-tuple-element.70), channel_id=1, source_target_pairs={{0,4},{1,5},{8,12},{9,13},{4,0},{5,1},{12,8},{13,9},{2,6},{3,7},{1... | collective-permute-start | bytes 1376264 | tf_op jit(solution)/shard_map/ppermute | solution.py:48
  36.4 5.2 %collective-permute-done.7.refs_4_ = f32[16,72,128]{2,1,0:T(8,128)S(1)} collective-permute-done((f32[16,72,128]{2,1,0:T(8,128)S(1)}, f32[16,72,128]{2,1,0:T(8,128)S(1)}, u32[]{:S(2)}, u32[]{:S(2)}) %collective-permute-start.7) | collective-permute-done | bytes 589856 | tf_op jit(solution)/shard_map/ppermute | solution.py:48
  42.8 3.2 %collective-permute-start.14 = (f32[16,72,128]{2,1,0:T(8,128)S(1)}, f32[16,72,128]{2,1,0:T(8,128)S(1)}, u32[]{:S(2)}, u32[]{:S(2)}) collective-permute-start(f32[16,72,128]{2,1,0:T(8,128)S(1)} %get-tuple-element.74), channel_id=1, source_target_pairs={{0,4},{1,5},{8,12},{9,13},{4,0},{5,1},{12,8},{13,9},{2,6},{3,7},{1... | collective-permute-start | bytes 1769480 | tf_op jit(solution)/shard_map/ppermute | solution.py:48
  47.5 4.0 %collective-permute-done.13.refs_6_ = f32[4,56,128]{2,1,0:T(8,128)S(1)} collective-permute-done((f32[4,56,128]{2,1,0:T(8,128)S(1)}, f32[4,56,128]{2,1,0:T(8,128)S(1)}, u32[]{:S(2)}, u32[]{:S(2)}) %collective-permute-start.13) | collective-permute-done | bytes 114720 | tf_op jit(solution)/shard_map/ppermute | solution.py:48
  52.5 3.2 %collective-permute-start.18 = (f32[16,56,128]{2,1,0:T(8,128)S(1)}, f32[16,56,128]{2,1,0:T(8,128)S(1)}, u32[]{:S(2)}, u32[]{:S(2)}) collective-permute-start(f32[16,56,128]{2,1,0:T(8,128)S(1)} %get-tuple-element.79), channel_id=1, source_target_pairs={{0,4},{1,5},{8,12},{9,13},{4,0},{5,1},{12,8},{13,9},{2,6},{3,7},{1... | collective-permute-start | bytes 1376264 | tf_op jit(solution)/shard_map/ppermute | solution.py:48
  57.2 2.4 %collective-permute-done.17.refs_7_ = f32[16,4,128]{2,1,0:T(4,128)S(1)} collective-permute-done((f32[16,4,128]{2,1,0:T(4,128)S(1)}, f32[16,4,128]{2,1,0:T(4,128)S(1)}, u32[]{:S(2)}, u32[]{:S(2)}) %collective-permute-start.17) | collective-permute-done | bytes 32800 | tf_op jit(solution)/shard_map/ppermute | solution.py:48
  61.1 3.9 %collective-permute-done.16.refs_6_ = f32[4,72,128]{2,1,0:T(8,128)S(1)} collective-permute-done((f32[4,72,128]{2,1,0:T(8,128)S(1)}, f32[4,72,128]{2,1,0:T(8,128)S(1)}, u32[]{:S(2)}, u32[]{:S(2)}) %collective-permute-start.16) | collective-permute-done | bytes 147488 | tf_op jit(solution)/shard_map/ppermute | solution.py:48
  66.1 2.3 %collective-permute-start.28 = (f32[16,72,128]{2,1,0:T(8,128)S(1)}, f32[16,72,128]{2,1,0:T(8,128)S(1)}, u32[]{:S(2)}, u32[]{:S(2)}) collective-permute-start(f32[16,72,128]{2,1,0:T(8,128)S(1)} %get-tuple-element.91), channel_id=1, source_target_pairs={{0,4},{1,5},{8,12},{9,13},{4,0},{5,1},{12,8},{13,9},{2,6},{3,7},{1... | collective-permute-start | bytes 1769480 | tf_op jit(solution)/shard_map/ppermute | solution.py:48
  70.0 4.0 %collective-permute-done.20.refs_6_ = f32[4,56,128]{2,1,0:T(8,128)S(1)} collective-permute-done((f32[4,56,128]{2,1,0:T(8,128)S(1)}, f32[4,56,128]{2,1,0:T(8,128)S(1)}, u32[]{:S(2)}, u32[]{:S(2)}) %collective-permute-start.20) | collective-permute-done | bytes 114720 | tf_op jit(solution)/shard_map/ppermute | solution.py:48
  75.0 2.0 %collective-permute-start.23 = (f32[4,56,128]{2,1,0:T(8,128)S(1)}, f32[4,56,128]{2,1,0:T(8,128)S(1)}, u32[]{:S(2)}, u32[]{:S(2)}) collective-permute-start(f32[4,56,128]{2,1,0:T(8,128)S(1)} %get-tuple-element.85), channel_id=1, source_target_pairs={{0,16},{1,17},{16,0},{17,1},{2,18},{3,19},{18,2},{19,3},{4,20},{5,... | collective-permute-start | bytes 344072 | tf_op jit(solution)/shard_map/ppermute | solution.py:48
  77.0 2.7 %collective-permute-start.26 = (f32[16,40,128]{2,1,0:T(8,128)S(1)}, f32[16,40,128]{2,1,0:T(8,128)S(1)}, u32[]{:S(2)}, u32[]{:S(2)}) collective-permute-start(f32[16,40,128]{2,1,0:T(8,128)S(1)} %get-tuple-element.89), channel_id=1, source_target_pairs={{0,4},{1,5},{8,12},{9,13},{4,0},{5,1},{12,8},{13,9},{2,6},{3,7},{1... | collective-permute-start | bytes 983048 | tf_op jit(solution)/shard_map/ppermute | solution.py:48
  81.2 2.4 %collective-permute-done.24.refs_7_.refs_6_ = f32[16,4,128]{2,1,0:T(4,128)S(1)} collective-permute-done((f32[16,4,128]{2,1,0:T(4,128)S(1)}, f32[16,4,128]{2,1,0:T(4,128)S(1)}, u32[]{:S(2)}, u32[]{:S(2)}) %collective-permute-start.24) | collective-permute-done | bytes 32800 | tf_op jit(solution)/shard_map/ppermute | solution.py:48
  84.1 4.7 %collective-permute-done.30.refs_4_.refs_6_ = f32[4,72,128]{2,1,0:T(8,128)S(1)} collective-permute-done((f32[4,72,128]{2,1,0:T(8,128)S(1)}, f32[4,72,128]{2,1,0:T(8,128)S(1)}, u32[]{:S(2)}, u32[]{:S(2)}) %collective-permute-start.30) | collective-permute-done | bytes 147488 | tf_op jit(solution)/shard_map/ppermute | solution.py:48
  93.6 2.0 %collective-permute-start.32 = (f32[2,2,72,128]{3,2,1,0:T(8,128)S(1)}, f32[2,2,72,128]{3,2,1,0:T(8,128)S(1)}, u32[]{:S(2)}, u32[]{:S(2)}) collective-permute-start(f32[2,2,72,128]{3,2,1,0:T(8,128)S(1)} %get-tuple-element.99.refs_1_), channel_id=1, source_target_pairs={{0,16},{16,0},{1,17},{17,1},{2,18},{18,2},{3,19},{19,3},{4,20},{20... | collective-permute-start | bytes 442376 | tf_op jit(solution)/shard_map/ppermute | solution.py:363
  97.0 2.0 %collective-permute-start.25 = (f32[2,2,16,128]{3,2,1,0:T(8,128)S(1)}, f32[2,2,16,128]{3,2,1,0:T(8,128)S(1)}, u32[]{:S(2)}, u32[]{:S(2)}) collective-permute-start(f32[2,2,16,128]{3,2,1,0:T(8,128)S(1)} %get-tuple-element.88.refs_1_), channel_id=1, source_target_pairs={{0,16},{16,0},{1,17},{17,1},{2,18},{18,2},{3,19},{19,3},{4,20},{20... | collective-permute-start | bytes 98312 | tf_op jit(solution)/shard_map/ppermute | solution.py:363
  99.0 1.8 %shard_map.63.refs_3_ = f32[16,4,128,128]{3,2,1,0:T(8,128)} custom-call(f32[16,2,128,128]{3,2,1,0:T(8,128)S(1)} %get-tuple-element.94.refs_8_.refs_0_, f32[2,2,128,128]{3,2,1,0:T(8,128)S(1)} %get-tuple-element.100.refs_1_, f32[2,2,128,128]{3,2,1,0:T(8,128)S(1)} %collective-permute-done.33.refs_2_), custom_call_target="tpu_custom_call" | custom-call | flops 5242880 | tf_op jit(solution)/shard_map/pallas_call | solution.py:23
  (61 shorter events, 31.8 us)
Async XLA Ops:
  1.9 17.3 %collective-permute-start = (f32[16,72,128]{2,1,0:T(8,128)S(1)}, f32[16,72,128]{2,1,0:T(8,128)S(1)}, u32[]{:S(2)}, u32[]{:S(2)}) collective-permute-start(f32[16,72,128]{2,1,0:T(8,128)S(1)} %get-tuple-element.56), channel_id=1, source_target_pairs={{0,4},{1,5},{8,12},{9,13},{4,0},{5,1},{12,8},{13,9},{2,6},{3,7},{1... | collective-permute-start | bytes 1769480 | tf_op jit(solution)/shard_map/ppermute | solution.py:48
  5.0 14.2 %collective-permute-start.1 = (f32[16,72,128]{2,1,0:T(8,128)S(1)}, f32[16,72,128]{2,1,0:T(8,128)S(1)}, u32[]{:S(2)}, u32[]{:S(2)}) collective-permute-start(f32[16,72,128]{2,1,0:T(8,128)S(1)} %get-tuple-element.57), channel_id=1, source_target_pairs={{4,8},{5,9},{0,1},{12,13},{8,4},{9,5},{1,0},{13,12},{6,10},{7,11},... | collective-permute-start | bytes 1769480 | tf_op jit(solution)/shard_map/ppermute | solution.py:48
  6.3 11.0 %collective-permute-start.2 = (f32[4,72,128]{2,1,0:T(8,128)S(1)}, f32[4,72,128]{2,1,0:T(8,128)S(1)}, u32[]{:S(2)}, u32[]{:S(2)}) collective-permute-start(f32[4,72,128]{2,1,0:T(8,128)S(1)} %get-tuple-element.58), channel_id=1, source_target_pairs={{0,16},{1,17},{16,0},{17,1},{2,18},{3,19},{18,2},{19,3},{4,20},{5,... | collective-permute-start | bytes 442376 | tf_op jit(solution)/shard_map/ppermute | solution.py:48
  7.9 9.3 %collective-permute-start.3 = (f32[16,4,128]{2,1,0:T(4,128)S(1)}, f32[16,4,128]{2,1,0:T(4,128)S(1)}, u32[]{:S(2)}, u32[]{:S(2)}) collective-permute-start(f32[16,4,128]{2,1,0:T(4,128)S(1)} %get-tuple-element.59), channel_id=1, source_target_pairs={{0,2},{1,3},{2,0},{3,1},{4,6},{5,7},{6,4},{7,5},{8,10},{9,11},{10,... | collective-permute-start | bytes 98312 | tf_op jit(solution)/shard_map/ppermute | solution.py:48
  9.4 21.7 %collective-permute-start.4 = (f32[16,56,128]{2,1,0:T(8,128)S(1)}, f32[16,56,128]{2,1,0:T(8,128)S(1)}, u32[]{:S(2)}, u32[]{:S(2)}) collective-permute-start(f32[16,56,128]{2,1,0:T(8,128)S(1)} %get-tuple-element.61), channel_id=1, source_target_pairs={{0,4},{1,5},{8,12},{9,13},{4,0},{5,1},{12,8},{13,9},{2,6},{3,7},{1... | collective-permute-start | bytes 1376264 | tf_op jit(solution)/shard_map/ppermute | solution.py:48
  17.2 13.9 %collective-permute-start.5 = (f32[16,56,128]{2,1,0:T(8,128)S(1)}, f32[16,56,128]{2,1,0:T(8,128)S(1)}, u32[]{:S(2)}, u32[]{:S(2)}) collective-permute-start(f32[16,56,128]{2,1,0:T(8,128)S(1)} %get-tuple-element.62), channel_id=1, source_target_pairs={{4,8},{5,9},{0,1},{12,13},{8,4},{9,5},{1,0},{13,12},{6,10},{7,11},... | collective-permute-start | bytes 1376264 | tf_op jit(solution)/shard_map/ppermute | solution.py:48
  20.8 20.8 %collective-permute-start.7 = (f32[16,72,128]{2,1,0:T(8,128)S(1)}, f32[16,72,128]{2,1,0:T(8,128)S(1)}, u32[]{:S(2)}, u32[]{:S(2)}) collective-permute-start(f32[16,72,128]{2,1,0:T(8,128)S(1)} %get-tuple-element.65), channel_id=1, source_target_pairs={{0,4},{1,5},{8,12},{9,13},{4,0},{5,1},{12,8},{13,9},{2,6},{3,7},{1... | collective-permute-start | bytes 1769480 | tf_op jit(solution)/shard_map/ppermute | solution.py:48
  24.0 17.6 %collective-permute-start.8 = (f32[16,72,128]{2,1,0:T(8,128)S(1)}, f32[16,72,128]{2,1,0:T(8,128)S(1)}, u32[]{:S(2)}, u32[]{:S(2)}) collective-permute-start(f32[16,72,128]{2,1,0:T(8,128)S(1)} %get-tuple-element.66), channel_id=1, source_target_pairs={{4,8},{5,9},{0,1},{12,13},{8,4},{9,5},{1,0},{13,12},{6,10},{7,11},... | collective-permute-start | bytes 1769480 | tf_op jit(solution)/shard_map/ppermute | solution.py:48
  29.6 6.8 %collective-permute-start.9 = (f32[4,72,128]{2,1,0:T(8,128)S(1)}, f32[4,72,128]{2,1,0:T(8,128)S(1)}, u32[]{:S(2)}, u32[]{:S(2)}) collective-permute-start(f32[4,72,128]{2,1,0:T(8,128)S(1)} %get-tuple-element.67), channel_id=1, source_target_pairs={{0,16},{1,17},{16,0},{17,1},{2,18},{3,19},{18,2},{19,3},{4,20},{5,... | collective-permute-start | bytes 442376 | tf_op jit(solution)/shard_map/ppermute | solution.py:48
  34.0 17.6 %collective-permute-start.11 = (f32[16,56,128]{2,1,0:T(8,128)S(1)}, f32[16,56,128]{2,1,0:T(8,128)S(1)}, u32[]{:S(2)}, u32[]{:S(2)}) collective-permute-start(f32[16,56,128]{2,1,0:T(8,128)S(1)} %get-tuple-element.70), channel_id=1, source_target_pairs={{0,4},{1,5},{8,12},{9,13},{4,0},{5,1},{12,8},{13,9},{2,6},{3,7},{1... | collective-permute-start | bytes 1376264 | tf_op jit(solution)/shard_map/ppermute | solution.py:48
  36.4 15.1 %collective-permute-start.12 = (f32[16,56,128]{2,1,0:T(8,128)S(1)}, f32[16,56,128]{2,1,0:T(8,128)S(1)}, u32[]{:S(2)}, u32[]{:S(2)}) collective-permute-start(f32[16,56,128]{2,1,0:T(8,128)S(1)} %get-tuple-element.71), channel_id=1, source_target_pairs={{4,8},{5,9},{0,1},{12,13},{8,4},{9,5},{1,0},{13,12},{6,10},{7,11},... | collective-permute-start | bytes 1376264 | tf_op jit(solution)/shard_map/ppermute | solution.py:48
  42.8 22.3 %collective-permute-start.14 = (f32[16,72,128]{2,1,0:T(8,128)S(1)}, f32[16,72,128]{2,1,0:T(8,128)S(1)}, u32[]{:S(2)}, u32[]{:S(2)}) collective-permute-start(f32[16,72,128]{2,1,0:T(8,128)S(1)} %get-tuple-element.74), channel_id=1, source_target_pairs={{0,4},{1,5},{8,12},{9,13},{4,0},{5,1},{12,8},{13,9},{2,6},{3,7},{1... | collective-permute-start | bytes 1769480 | tf_op jit(solution)/shard_map/ppermute | solution.py:48
  46.0 19.0 %collective-permute-start.15 = (f32[16,72,128]{2,1,0:T(8,128)S(1)}, f32[16,72,128]{2,1,0:T(8,128)S(1)}, u32[]{:S(2)}, u32[]{:S(2)}) collective-permute-start(f32[16,72,128]{2,1,0:T(8,128)S(1)} %get-tuple-element.75), channel_id=1, source_target_pairs={{4,8},{5,9},{0,1},{12,13},{8,4},{9,5},{1,0},{13,12},{6,10},{7,11},... | collective-permute-start | bytes 1769480 | tf_op jit(solution)/shard_map/ppermute | solution.py:48
  52.5 21.5 %collective-permute-start.18 = (f32[16,56,128]{2,1,0:T(8,128)S(1)}, f32[16,56,128]{2,1,0:T(8,128)S(1)}, u32[]{:S(2)}, u32[]{:S(2)}) collective-permute-start(f32[16,56,128]{2,1,0:T(8,128)S(1)} %get-tuple-element.79), channel_id=1, source_target_pairs={{0,4},{1,5},{8,12},{9,13},{4,0},{5,1},{12,8},{13,9},{2,6},{3,7},{1... | collective-permute-start | bytes 1376264 | tf_op jit(solution)/shard_map/ppermute | solution.py:48
  55.7 18.3 %collective-permute-start.19 = (f32[16,56,128]{2,1,0:T(8,128)S(1)}, f32[16,56,128]{2,1,0:T(8,128)S(1)}, u32[]{:S(2)}, u32[]{:S(2)}) collective-permute-start(f32[16,56,128]{2,1,0:T(8,128)S(1)} %get-tuple-element.80), channel_id=1, source_target_pairs={{4,8},{5,9},{0,1},{12,13},{8,4},{9,5},{1,0},{13,12},{6,10},{7,11},... | collective-permute-start | bytes 1376264 | tf_op jit(solution)/shard_map/ppermute | solution.py:48
  66.1 24.5 %collective-permute-start.28 = (f32[16,72,128]{2,1,0:T(8,128)S(1)}, f32[16,72,128]{2,1,0:T(8,128)S(1)}, u32[]{:S(2)}, u32[]{:S(2)}) collective-permute-start(f32[16,72,128]{2,1,0:T(8,128)S(1)} %get-tuple-element.91), channel_id=1, source_target_pairs={{0,4},{1,5},{8,12},{9,13},{4,0},{5,1},{12,8},{13,9},{2,6},{3,7},{1... | collective-permute-start | bytes 1769480 | tf_op jit(solution)/shard_map/ppermute | solution.py:48
  68.5 22.2 %collective-permute-start.29 = (f32[16,72,128]{2,1,0:T(8,128)S(1)}, f32[16,72,128]{2,1,0:T(8,128)S(1)}, u32[]{:S(2)}, u32[]{:S(2)}) collective-permute-start(f32[16,72,128]{2,1,0:T(8,128)S(1)} %get-tuple-element.92), channel_id=1, source_target_pairs={{4,8},{5,9},{0,1},{12,13},{8,4},{9,5},{1,0},{13,12},{6,10},{7,11},... | collective-permute-start | bytes 1769480 | tf_op jit(solution)/shard_map/ppermute | solution.py:48
  75.0 9.1 %collective-permute-start.23 = (f32[4,56,128]{2,1,0:T(8,128)S(1)}, f32[4,56,128]{2,1,0:T(8,128)S(1)}, u32[]{:S(2)}, u32[]{:S(2)}) collective-permute-start(f32[4,56,128]{2,1,0:T(8,128)S(1)} %get-tuple-element.85), channel_id=1, source_target_pairs={{0,16},{1,17},{16,0},{17,1},{2,18},{3,19},{18,2},{19,3},{4,20},{5,... | collective-permute-start | bytes 344072 | tf_op jit(solution)/shard_map/ppermute | solution.py:48
  77.0 16.7 %collective-permute-start.26 = (f32[16,40,128]{2,1,0:T(8,128)S(1)}, f32[16,40,128]{2,1,0:T(8,128)S(1)}, u32[]{:S(2)}, u32[]{:S(2)}) collective-permute-start(f32[16,40,128]{2,1,0:T(8,128)S(1)} %get-tuple-element.89), channel_id=1, source_target_pairs={{0,4},{1,5},{8,12},{9,13},{4,0},{5,1},{12,8},{13,9},{2,6},{3,7},{1... | collective-permute-start | bytes 983048 | tf_op jit(solution)/shard_map/ppermute | solution.py:48
  84.1 11.5 %collective-permute-start.27 = (f32[16,40,128]{2,1,0:T(8,128)S(1)}, f32[16,40,128]{2,1,0:T(8,128)S(1)}, u32[]{:S(2)}, u32[]{:S(2)}) collective-permute-start(f32[16,40,128]{2,1,0:T(8,128)S(1)} %get-tuple-element.90), channel_id=1, source_target_pairs={{4,8},{5,9},{0,1},{12,13},{8,4},{9,5},{1,0},{13,12},{6,10},{7,11},... | collective-permute-start | bytes 983048 | tf_op jit(solution)/shard_map/ppermute | solution.py:48
  90.2 8.8 %collective-permute-start.33 = (f32[2,2,128,128]{3,2,1,0:T(8,128)S(1)}, f32[2,2,128,128]{3,2,1,0:T(8,128)S(1)}, u32[]{:S(2)}, u32[]{:S(2)}) collective-permute-start(f32[2,2,128,128]{3,2,1,0:T(8,128)S(1)} %get-tuple-element.100.refs_1_), channel_id=1, source_target_pairs={{0,16},{16,0},{1,17},{17,1},{2,18},{18,2},{3,19},{19,3},{4,20},{20... | collective-permute-start | bytes 786440 | tf_op jit(solution)/shard_map/ppermute | solution.py:363
  90.7 6.1 %collective-permute-start.21 = (f32[16,16,128]{2,1,0:T(8,128)S(1)}, f32[16,16,128]{2,1,0:T(8,128)S(1)}, u32[]{:S(2)}, u32[]{:S(2)}) collective-permute-start(f32[16,16,128]{2,1,0:T(8,128)S(1)} %get-tuple-element.83), channel_id=1, source_target_pairs={{0,4},{1,5},{8,12},{9,13},{4,0},{5,1},{12,8},{13,9},{2,6},{3,7},{1... | collective-permute-start | bytes 393224 | tf_op jit(solution)/shard_map/ppermute | solution.py:48
  93.6 7.4 %collective-permute-start.32 = (f32[2,2,72,128]{3,2,1,0:T(8,128)S(1)}, f32[2,2,72,128]{3,2,1,0:T(8,128)S(1)}, u32[]{:S(2)}, u32[]{:S(2)}) collective-permute-start(f32[2,2,72,128]{3,2,1,0:T(8,128)S(1)} %get-tuple-element.99.refs_1_), channel_id=1, source_target_pairs={{0,16},{16,0},{1,17},{17,1},{2,18},{18,2},{3,19},{19,3},{4,20},{20... | collective-permute-start | bytes 442376 | tf_op jit(solution)/shard_map/ppermute | solution.py:363
  97.0 6.4 %collective-permute-start.25 = (f32[2,2,16,128]{3,2,1,0:T(8,128)S(1)}, f32[2,2,16,128]{3,2,1,0:T(8,128)S(1)}, u32[]{:S(2)}, u32[]{:S(2)}) collective-permute-start(f32[2,2,16,128]{3,2,1,0:T(8,128)S(1)} %get-tuple-element.88.refs_1_), channel_id=1, source_target_pairs={{0,16},{16,0},{1,17},{17,1},{2,18},{18,2},{3,19},{19,3},{4,20},{20... | collective-permute-start | bytes 98312 | tf_op jit(solution)/shard_map/ppermute | solution.py:363
  (10 other events, 50.8 us)

commit v2 on v1

--- a/solution.py
+++ b/solution.py
@@ -7,8 +7,8 @@
 
 
 STEPS = 4
-CHUNKS = (9, 7)
-LAST_CUT = (5, 2)
+CHUNKS = (11, 5)
+LAST_CUT = (3, 2)
 ROWS = 8
 HBM = pl.BlockSpec(memory_space=pltpu.HBM)
 VMEM = pl.BlockSpec(memory_space=pltpu.VMEM)
@@ -302,49 +302,58 @@
     return new, z, y, outs
 
 
-def finish(new, own, others, layers, span, anomaly, field, shape):
+def finish(jobs, anomaly, field, shape):
     J, _, _, L = shape
-    k0, kc = span
-    nl = len(layers)
-    count = len(others) + 1
     buffers = [buffer for buffer in (anomaly, field) if buffer is not None]
     outs_count = 1 if field is None else 2
+    ins, scratch = [], []
+    for new, own, others, layers, (k0, kc) in jobs:
+        ins += [new, own] + list(others)
+        scratch += [pltpu.VMEM((J, len(layers), kc, L), F32), pltpu.SemaphoreType.DMA((2, len(layers)))]
 
     def body(*refs):
-        u, sums = refs[0], refs[1 : 1 + count]
-        outs = refs[1 + count + len(buffers) : 1 + count + len(buffers) + outs_count]
-        scaled, sems = refs[-2:]
+        refs = list(refs)
+        cells = []
+        for _, _, others, _, _ in jobs:
+            cells.append((refs.pop(0), [refs.pop(0) for _ in range(1 + len(others))]))
+        for _ in buffers:
+            refs.pop(0)
+        outs = [refs.pop(0) for _ in range(outs_count)]
         copies = []
         if field is not None:
-            copies += write_copies(u, outs[1], layers, k0, kc, sems.at[1])
+            for n, ((u, _), (*_, layers, (k0, kc))) in enumerate(zip(cells, jobs)):
+                copies += write_copies(u, outs[1], layers, k0, kc, refs[2 * n + 1].at[1])
             for copy in copies:
                 copy.start()
-        results = write_copies(scaled, outs[0], layers, k0, kc, sems.at[0])
-        for n in range(nl):
-
-            def tile(t, carry, n=n):
-                here = pl.ds(pl.multiple_of(t * ROWS, ROWS), ROWS)
-                means = [ref[0, n, here] for ref in sums]
-                mean = means[0]
-                for other in means[1:]:
-                    mean = mean + other
-                mean = mean * (1.0 / count)
-                spread = None
-                for ref, own_mean in zip(sums, means):
-                    off = own_mean - mean
-                    part = ref[1, n, here] + J * (off * off)
-                    spread = part if spread is None else spread + part
-                scale = lax.rsqrt(spread * (1.0 / (J * count)) + 0.0001)
-                for j in range(J):
-                    scaled[j, n, here] = (u[j, n, here] - mean) * scale
-                return carry
-
-            lax.fori_loop(0, kc // ROWS, tile, 0)
-            results[n].start()
-        for copy in copies + results:
+        for m, ((u, sums), (*_, layers, (k0, kc))) in enumerate(zip(cells, jobs)):
+            scaled, sems = refs[2 * m], refs[2 * m + 1]
+            results = write_copies(scaled, outs[0], layers, k0, kc, sems.at[0])
+            for n in range(len(layers)):
+
+                def tile(t, carry, n=n, u=u, sums=sums, scaled=scaled):
+                    here = pl.ds(pl.multiple_of(t * ROWS, ROWS), ROWS)
+                    count = len(sums)
+                    means = [ref[0, n, here] for ref in sums]
+                    mean = means[0]
+                    for other in means[1:]:
+                        mean = mean + other
+                    mean = mean * (1.0 / count)
+                    spread = None
+                    for ref, own_mean in zip(sums, means):
+                        off = own_mean - mean
+                        part = ref[1, n, here] + J * (off * off)
+                        spread = part if spread is None else spread + part
+                    scale = lax.rsqrt(spread * (1.0 / (J * count)) + 0.0001)
+                    for j in range(J):
+                        scaled[j, n, here] = (u[j, n, here] - mean) * scale
+                    return carry
+
+                lax.fori_loop(0, kc // ROWS, tile, 0)
+                results[n].start()
+            copies += results
+        for copy in copies:
             copy.wait()
 
-    ins = [new, own] + list(others)
     aliases = {len(ins) + n: (n if anomaly is not None else 1) for n in range(len(buffers))}
     return call(
         body,
@@ -352,9 +361,9 @@
         [VMEM] * len(ins) + [HBM] * len(buffers),
         [jax.ShapeDtypeStruct(shape, F32)] * outs_count,
         [HBM] * outs_count,
-        [pltpu.VMEM((J, nl, kc, L), F32), pltpu.SemaphoreType.DMA((2, nl))],
+        scratch,
         aliases,
-        flops=10 * J * nl * kc * L,
+        flops=sum(10 * J * len(layers) * kc * L for *_, layers, (_, kc) in jobs),
     )
 
 
@@ -430,13 +439,13 @@
         field = field if wrote is None else wrote
         others = other_rows(own)
         span = (pieces[0][1], sum(piece[2] for piece in pieces))
-        write = (new, layers, span, field) if n < len(jobs) - 2 else None
+        write = (new, layers, span, field) if n == 0 else None
         sums.append((new, own, others, layers, span))
-    for n, job in enumerate(sums):
-        to_field = field if n >= len(sums) - 2 else None
-        done = finish(*job, anomaly, to_field, shape)
-        anomaly = done[0]
-        field = done[1] if to_field is not None else field
+    for n, group in enumerate(([sums[0]], [sums[1]], sums[2:])):
+        if group:
+            done = finish(group, anomaly, field if n > 0 else None, shape)
+            anomaly = done[0]
+            field = done[1] if n > 0 else field
     return anomaly, field
 
 

time: 104 us -> 132 us (1.27)
  waiting for transfers between devices: 34.6 us -> 64.1 us
    ppermute x30, waiting for transfers between devices: 34.3 us -> 64.1 us  [exchange(): lax.ppermute(buffer, (axis, 'trial'), pairs + [(b, a) for a, b in pairs])]
    pallas_call x17 -> x16, Pallas kernels: 23.1 us -> 21.8 us  [call(): pl.pallas_call(body, in_specs=in_specs, out_shape=outs, out_specs=out_spe...]
  transfers between devices with their start and end apart: 34 -> 34, of which waited for: 11 -> 12; matrix products, arithmetic and copies ran while one was open for 0% -> 0% of each run, Pallas kernels for 20% -> 11%
where the time goes in v2:
time: 132 us
  waiting for transfers between devices  64.1 us (49%)
  starting transfers between devices  45 us (34%)
  Pallas kernels  21.8 us (17%)
    ppermute x30, waiting for transfers between devices, exchange(): lax.ppermute(buffer, (axis, 'trial'), pairs + [(b, a) for a, b in pairs])  64.1 us
    ppermute x30, starting transfers between devices, exchange(): lax.ppermute(buffer, (axis, 'trial'), pairs + [(b, a) for a, b in pairs])  40.3 us
    pallas_call x16, Pallas kernels, call(): pl.pallas_call(body, in_specs=in_specs, out_shape=outs, out_specs=out_spe...  21.8 us
    ppermute x4, starting transfers between devices, other_rows(): lax.ppermute(own, 'rows', [(i, (i + shift) % count) for i in range(count)])  4.65 us
  transfers between devices with their start and end apart: 34, of which 12 were waited for; matrix products, arithmetic and copies ran while one was open for 0% of the time, Pallas kernels for 11%

profile of v2, /device:TPU:0, one launch (start us, length us, event | category | flops | bytes accessed | tf_op | source)
XLA Modules:
  0.0 131.7 jit_solution(15729641865503394033)
XLA Ops:
  2.0 3.1 %collective-permute-start = (f32[16,88,128]{2,1,0:T(8,128)S(1)}, f32[16,88,128]{2,1,0:T(8,128)S(1)}, u32[]{:S(2)}, u32[]{:S(2)}) collective-permute-start(f32[16,88,128]{2,1,0:T(8,128)S(1)} %get-tuple-element.55), channel_id=1, source_target_pairs={{0,4},{1,5},{8,12},{9,13},{4,0},{5,1},{12,8},{13,9},{2,6},{3,7},{1... | collective-permute-start | bytes 2162696 | tf_op jit(solution)/shard_map/ppermute | solution.py:48
  9.4 4.7 %shard_map.50 = (f32[16,4,128,128]{3,2,1,0:T(8,128)S(1)}, f32[16,4,128,128]{3,2,1,0:T(8,128)S(1)}, f32[16,4,128,128]{3,2,1,0:T(8,128)S(1)}) custom-call(f32[16,4,128,128]{3,2,1,0:T(8,128)} %u.3, f32[16,4,128,128]{3,2,1,0:T(8,128)} %refs_1_.1, f32[16,4,128,128]{3,2,1,0:T(8,128)} %refs_2_.1), custom_call_target="tpu_custom_call" | custom-call | tf_op jit(solution)/shard_map/pallas_call | solution.py:23
  14.1 7.2 %collective-permute-done.refs_3_ = f32[16,88,128]{2,1,0:T(8,128)S(1)} collective-permute-done((f32[16,88,128]{2,1,0:T(8,128)S(1)}, f32[16,88,128]{2,1,0:T(8,128)S(1)}, u32[]{:S(2)}, u32[]{:S(2)}) %collective-permute-start) | collective-permute-done | bytes 720928 | tf_op jit(solution)/shard_map/ppermute | solution.py:48
  21.3 2.0 %shard_map.53 = (f32[16,4,88,128]{3,2,1,0:T(8,128)S(1)}, f32[16,88,128]{2,1,0:T(8,128)S(1)}, f32[16,88,128]{2,1,0:T(8,128)S(1)}, f32[4,88,128]{2,1,0:T(8,128)S(1)}) custom-call(f32[16,4,128,128]{3,2,1,0:T(8,128)S(1)} %get-tuple-element.52.refs_0_, f32[16,4,128,128]{3,2,1,0:T(8,128)S(1)} %get-tuple-element.53.refs_1_, ...), custom_call_target="tpu_custom_call" | custom-call | flops 7208960 | tf_op jit(solution)/shard_map/pallas_call | solution.py:23
  23.2 2.9 %collective-permute-start.7 = (f32[16,88,128]{2,1,0:T(8,128)S(1)}, f32[16,88,128]{2,1,0:T(8,128)S(1)}, u32[]{:S(2)}, u32[]{:S(2)}) collective-permute-start(f32[16,88,128]{2,1,0:T(8,128)S(1)} %get-tuple-element.64), channel_id=1, source_target_pairs={{0,4},{1,5},{8,12},{9,13},{4,0},{5,1},{12,8},{13,9},{2,6},{3,7},{1... | collective-permute-start | bytes 2162696 | tf_op jit(solution)/shard_map/ppermute | solution.py:48
  26.2 2.0 %collective-permute-start.4 = (f32[16,40,128]{2,1,0:T(8,128)S(1)}, f32[16,40,128]{2,1,0:T(8,128)S(1)}, u32[]{:S(2)}, u32[]{:S(2)}) collective-permute-start(f32[16,40,128]{2,1,0:T(8,128)S(1)} %get-tuple-element.60), channel_id=1, source_target_pairs={{0,4},{1,5},{8,12},{9,13},{4,0},{5,1},{12,8},{13,9},{2,6},{3,7},{1... | collective-permute-start | bytes 983048 | tf_op jit(solution)/shard_map/ppermute | solution.py:48
  29.7 3.3 %collective-permute-done.6.refs_5_ = f32[4,40,128]{2,1,0:T(8,128)S(1)} collective-permute-done((f32[4,40,128]{2,1,0:T(8,128)S(1)}, f32[4,40,128]{2,1,0:T(8,128)S(1)}, u32[]{:S(2)}, u32[]{:S(2)}) %collective-permute-start.6) | collective-permute-done | bytes 81952 | tf_op jit(solution)/shard_map/ppermute | solution.py:48
  34.6 13.9 %collective-permute-done.4.refs_3_ = f32[16,40,128]{2,1,0:T(8,128)S(1)} collective-permute-done((f32[16,40,128]{2,1,0:T(8,128)S(1)}, f32[16,40,128]{2,1,0:T(8,128)S(1)}, u32[]{:S(2)}, u32[]{:S(2)}) %collective-permute-start.4) | collective-permute-done | bytes 327712 | tf_op jit(solution)/shard_map/ppermute | solution.py:48
  51.0 2.4 %collective-permute-done.10.refs_7_ = f32[16,4,128]{2,1,0:T(4,128)S(1)} collective-permute-done((f32[16,4,128]{2,1,0:T(4,128)S(1)}, f32[16,4,128]{2,1,0:T(4,128)S(1)}, u32[]{:S(2)}, u32[]{:S(2)}) %collective-permute-start.10) | collective-permute-done | bytes 32800 | tf_op jit(solution)/shard_map/ppermute | solution.py:48
  54.7 1.9 %collective-permute-start.14 = (f32[16,88,128]{2,1,0:T(8,128)S(1)}, f32[16,88,128]{2,1,0:T(8,128)S(1)}, u32[]{:S(2)}, u32[]{:S(2)}) collective-permute-start(f32[16,88,128]{2,1,0:T(8,128)S(1)} %get-tuple-element.73), channel_id=1, source_target_pairs={{0,4},{1,5},{8,12},{9,13},{4,0},{5,1},{12,8},{13,9},{2,6},{3,7},{1... | collective-permute-start | bytes 2162696 | tf_op jit(solution)/shard_map/ppermute | solution.py:48
  56.6 1.9 %collective-permute-start.11 = (f32[16,40,128]{2,1,0:T(8,128)S(1)}, f32[16,40,128]{2,1,0:T(8,128)S(1)}, u32[]{:S(2)}, u32[]{:S(2)}) collective-permute-start(f32[16,40,128]{2,1,0:T(8,128)S(1)} %get-tuple-element.69), channel_id=1, source_target_pairs={{0,4},{1,5},{8,12},{9,13},{4,0},{5,1},{12,8},{13,9},{2,6},{3,7},{1... | collective-permute-start | bytes 983048 | tf_op jit(solution)/shard_map/ppermute | solution.py:48
  60.1 3.3 %collective-permute-done.13.refs_6_ = f32[4,40,128]{2,1,0:T(8,128)S(1)} collective-permute-done((f32[4,40,128]{2,1,0:T(8,128)S(1)}, f32[4,40,128]{2,1,0:T(8,128)S(1)}, u32[]{:S(2)}, u32[]{:S(2)}) %collective-permute-start.13) | collective-permute-done | bytes 81952 | tf_op jit(solution)/shard_map/ppermute | solution.py:48
  65.0 12.2 %collective-permute-done.11.refs_4_ = f32[16,40,128]{2,1,0:T(8,128)S(1)} collective-permute-done((f32[16,40,128]{2,1,0:T(8,128)S(1)}, f32[16,40,128]{2,1,0:T(8,128)S(1)}, u32[]{:S(2)}, u32[]{:S(2)}) %collective-permute-start.11) | collective-permute-done | bytes 327712 | tf_op jit(solution)/shard_map/ppermute | solution.py:48
  79.4 2.4 %collective-permute-done.17.refs_7_ = f32[16,4,128]{2,1,0:T(4,128)S(1)} collective-permute-done((f32[16,4,128]{2,1,0:T(4,128)S(1)}, f32[16,4,128]{2,1,0:T(4,128)S(1)}, u32[]{:S(2)}, u32[]{:S(2)}) %collective-permute-start.17) | collective-permute-done | bytes 32800 | tf_op jit(solution)/shard_map/ppermute | solution.py:48
  83.2 1.8 %collective-permute-start.29 = (f32[16,88,128]{2,1,0:T(8,128)S(1)}, f32[16,88,128]{2,1,0:T(8,128)S(1)}, u32[]{:S(2)}, u32[]{:S(2)}) collective-permute-start(f32[16,88,128]{2,1,0:T(8,128)S(1)} %get-tuple-element.92), channel_id=1, source_target_pairs={{0,4},{1,5},{8,12},{9,13},{4,0},{5,1},{12,8},{13,9},{2,6},{3,7},{1... | collective-permute-start | bytes 2162696 | tf_op jit(solution)/shard_map/ppermute | solution.py:48
  85.0 1.7 %collective-permute-start.18 = (f32[16,40,128]{2,1,0:T(8,128)S(1)}, f32[16,40,128]{2,1,0:T(8,128)S(1)}, u32[]{:S(2)}, u32[]{:S(2)}) collective-permute-start(f32[16,40,128]{2,1,0:T(8,128)S(1)} %get-tuple-element.78), channel_id=1, source_target_pairs={{0,4},{1,5},{8,12},{9,13},{4,0},{5,1},{12,8},{13,9},{2,6},{3,7},{1... | collective-permute-start | bytes 983048 | tf_op jit(solution)/shard_map/ppermute | solution.py:48
  88.2 3.3 %collective-permute-done.20.refs_6_ = f32[4,40,128]{2,1,0:T(8,128)S(1)} collective-permute-done((f32[4,40,128]{2,1,0:T(8,128)S(1)}, f32[4,40,128]{2,1,0:T(8,128)S(1)}, u32[]{:S(2)}, u32[]{:S(2)}) %collective-permute-start.20) | collective-permute-done | bytes 81952 | tf_op jit(solution)/shard_map/ppermute | solution.py:48
  93.1 11.5 %collective-permute-done.18.refs_4_ = f32[16,40,128]{2,1,0:T(8,128)S(1)} collective-permute-done((f32[16,40,128]{2,1,0:T(8,128)S(1)}, f32[16,40,128]{2,1,0:T(8,128)S(1)}, u32[]{:S(2)}, u32[]{:S(2)}) %collective-permute-start.18) | collective-permute-done | bytes 327712 | tf_op jit(solution)/shard_map/ppermute | solution.py:48
  105.3 2.5 %collective-permute-start.24 = (f32[16,4,128]{2,1,0:T(4,128)S(1)}, f32[16,4,128]{2,1,0:T(4,128)S(1)}, u32[]{:S(2)}, u32[]{:S(2)}) collective-permute-start(f32[16,4,128]{2,1,0:T(4,128)S(1)} %get-tuple-element.85), channel_id=1, source_target_pairs={{0,2},{1,3},{2,0},{3,1},{4,6},{5,7},{6,4},{7,5},{8,10},{9,11},{10,... | collective-permute-start | bytes 98312 | tf_op jit(solution)/shard_map/ppermute | solution.py:48
  107.8 1.7 %collective-permute-start.21 = (f32[16,24,128]{2,1,0:T(8,128)S(1)}, f32[16,24,128]{2,1,0:T(8,128)S(1)}, u32[]{:S(2)}, u32[]{:S(2)}) collective-permute-start(f32[16,24,128]{2,1,0:T(8,128)S(1)} %get-tuple-element.82), channel_id=1, source_target_pairs={{0,4},{1,5},{8,12},{9,13},{4,0},{5,1},{12,8},{13,9},{2,6},{3,7},{1... | collective-permute-start | bytes 589832 | tf_op jit(solution)/shard_map/ppermute | solution.py:48
  111.2 2.9 %collective-permute-done.23.refs_6_.refs_5_ = f32[4,40,128]{2,1,0:T(8,128)S(1)} collective-permute-done((f32[4,40,128]{2,1,0:T(8,128)S(1)}, f32[4,40,128]{2,1,0:T(8,128)S(1)}, u32[]{:S(2)}, u32[]{:S(2)}) %collective-permute-start.23) | collective-permute-done | bytes 81952 | tf_op jit(solution)/shard_map/ppermute | solution.py:48
  119.0 3.8 %collective-permute-start.26 = (f32[16,16,128]{2,1,0:T(8,128)S(1)}, f32[16,16,128]{2,1,0:T(8,128)S(1)}, u32[]{:S(2)}, u32[]{:S(2)}) collective-permute-start(f32[16,16,128]{2,1,0:T(8,128)S(1)} %get-tuple-element.88), channel_id=1, source_target_pairs={{0,4},{1,5},{8,12},{9,13},{4,0},{5,1},{12,8},{13,9},{2,6},{3,7},{1... | collective-permute-start | bytes 393224 | tf_op jit(solution)/shard_map/ppermute | solution.py:48
  127.2 1.8 %shard_map.63.refs_3_ = f32[16,4,128,128]{3,2,1,0:T(8,128)} custom-call(f32[16,2,128,128]{3,2,1,0:T(8,128)S(1)} %get-tuple-element.95.refs_8_.refs_0_, f32[2,2,128,128]{3,2,1,0:T(8,128)S(1)} %get-tuple-element.98.refs_1_, f32[2,2,128,128]{3,2,1,0:T(8,128)S(1)} %collective-permute-done.33.refs_2_), custom_call_target="tpu_custom_call" | custom-call | flops 5242880 | tf_op jit(solution)/shard_map/pallas_call | solution.py:23
  128.9 1.6 %shard_map.64 = (f32[16,4,128,128]{3,2,1,0:T(8,128)}, f32[16,4,128,128]{3,2,1,0:T(8,128)}) custom-call(f32[16,2,88,128]{3,2,1,0:T(8,128)S(1)} %get-tuple-element.96.refs_0_, f32[2,2,88,128]{3,2,1,0:T(8,128)S(1)} %get-tuple-element.97.refs_1_, f32[2,2,88,128]{3,2,1,0:T(8,128)S(1)} %collective-permute-done.32.refs_2_, ...), custom_call_target="tpu_custom_call", output_to_operand_aliasing={{0}: (3, {}), {1}: (4, {})} | custom-call | flops 3604480 | tf_op jit(solution)/shard_map/pallas_call | solution.py:23
  (60 shorter events, 34.9 us)
Async XLA Ops:
  2.0 19.3 %collective-permute-start = (f32[16,88,128]{2,1,0:T(8,128)S(1)}, f32[16,88,128]{2,1,0:T(8,128)S(1)}, u32[]{:S(2)}, u32[]{:S(2)}) collective-permute-start(f32[16,88,128]{2,1,0:T(8,128)S(1)} %get-tuple-element.55), channel_id=1, source_target_pairs={{0,4},{1,5},{8,12},{9,13},{4,0},{5,1},{12,8},{13,9},{2,6},{3,7},{1... | collective-permute-start | bytes 2162696 | tf_op jit(solution)/shard_map/ppermute | solution.py:48
  5.1 16.1 %collective-permute-start.1 = (f32[16,88,128]{2,1,0:T(8,128)S(1)}, f32[16,88,128]{2,1,0:T(8,128)S(1)}, u32[]{:S(2)}, u32[]{:S(2)}) collective-permute-start(f32[16,88,128]{2,1,0:T(8,128)S(1)} %get-tuple-element.56), channel_id=1, source_target_pairs={{4,8},{5,9},{0,1},{12,13},{8,4},{9,5},{1,0},{13,12},{6,10},{7,11},... | collective-permute-start | bytes 2162696 | tf_op jit(solution)/shard_map/ppermute | solution.py:48
  6.3 7.8 %collective-permute-start.2 = (f32[4,88,128]{2,1,0:T(8,128)S(1)}, f32[4,88,128]{2,1,0:T(8,128)S(1)}, u32[]{:S(2)}, u32[]{:S(2)}) collective-permute-start(f32[4,88,128]{2,1,0:T(8,128)S(1)} %get-tuple-element.57), channel_id=1, source_target_pairs={{0,16},{1,17},{16,0},{17,1},{2,18},{3,19},{18,2},{19,3},{4,20},{5,... | collective-permute-start | bytes 540680 | tf_op jit(solution)/shard_map/ppermute | solution.py:48
  7.9 6.2 %collective-permute-start.3 = (f32[16,4,128]{2,1,0:T(4,128)S(1)}, f32[16,4,128]{2,1,0:T(4,128)S(1)}, u32[]{:S(2)}, u32[]{:S(2)}) collective-permute-start(f32[16,4,128]{2,1,0:T(4,128)S(1)} %get-tuple-element.58), channel_id=1, source_target_pairs={{0,2},{1,3},{2,0},{3,1},{4,6},{5,7},{6,4},{7,5},{8,10},{9,11},{10,... | collective-permute-start | bytes 98312 | tf_op jit(solution)/shard_map/ppermute | solution.py:48
  23.2 30.2 %collective-permute-start.7 = (f32[16,88,128]{2,1,0:T(8,128)S(1)}, f32[16,88,128]{2,1,0:T(8,128)S(1)}, u32[]{:S(2)}, u32[]{:S(2)}) collective-permute-start(f32[16,88,128]{2,1,0:T(8,128)S(1)} %get-tuple-element.64), channel_id=1, source_target_pairs={{0,4},{1,5},{8,12},{9,13},{4,0},{5,1},{12,8},{13,9},{2,6},{3,7},{1... | collective-permute-start | bytes 2162696 | tf_op jit(solution)/shard_map/ppermute | solution.py:48
  26.2 27.2 %collective-permute-start.8 = (f32[16,88,128]{2,1,0:T(8,128)S(1)}, f32[16,88,128]{2,1,0:T(8,128)S(1)}, u32[]{:S(2)}, u32[]{:S(2)}) collective-permute-start(f32[16,88,128]{2,1,0:T(8,128)S(1)} %get-tuple-element.65), channel_id=1, source_target_pairs={{4,8},{5,9},{0,1},{12,13},{8,4},{9,5},{1,0},{13,12},{6,10},{7,11},... | collective-permute-start | bytes 2162696 | tf_op jit(solution)/shard_map/ppermute | solution.py:48
  26.2 22.3 %collective-permute-start.4 = (f32[16,40,128]{2,1,0:T(8,128)S(1)}, f32[16,40,128]{2,1,0:T(8,128)S(1)}, u32[]{:S(2)}, u32[]{:S(2)}) collective-permute-start(f32[16,40,128]{2,1,0:T(8,128)S(1)} %get-tuple-element.60), channel_id=1, source_target_pairs={{0,4},{1,5},{8,12},{9,13},{4,0},{5,1},{12,8},{13,9},{2,6},{3,7},{1... | collective-permute-start | bytes 983048 | tf_op jit(solution)/shard_map/ppermute | solution.py:48
  28.2 20.3 %collective-permute-start.5 = (f32[16,40,128]{2,1,0:T(8,128)S(1)}, f32[16,40,128]{2,1,0:T(8,128)S(1)}, u32[]{:S(2)}, u32[]{:S(2)}) collective-permute-start(f32[16,40,128]{2,1,0:T(8,128)S(1)} %get-tuple-element.61), channel_id=1, source_target_pairs={{4,8},{5,9},{0,1},{12,13},{8,4},{9,5},{1,0},{13,12},{6,10},{7,11},... | collective-permute-start | bytes 983048 | tf_op jit(solution)/shard_map/ppermute | solution.py:48
  33.1 20.4 %collective-permute-start.9 = (f32[4,88,128]{2,1,0:T(8,128)S(1)}, f32[4,88,128]{2,1,0:T(8,128)S(1)}, u32[]{:S(2)}, u32[]{:S(2)}) collective-permute-start(f32[4,88,128]{2,1,0:T(8,128)S(1)} %get-tuple-element.66), channel_id=1, source_target_pairs={{0,16},{1,17},{16,0},{17,1},{2,18},{3,19},{18,2},{19,3},{4,20},{5,... | collective-permute-start | bytes 540680 | tf_op jit(solution)/shard_map/ppermute | solution.py:48
  54.7 27.1 %collective-permute-start.14 = (f32[16,88,128]{2,1,0:T(8,128)S(1)}, f32[16,88,128]{2,1,0:T(8,128)S(1)}, u32[]{:S(2)}, u32[]{:S(2)}) collective-permute-start(f32[16,88,128]{2,1,0:T(8,128)S(1)} %get-tuple-element.73), channel_id=1, source_target_pairs={{0,4},{1,5},{8,12},{9,13},{4,0},{5,1},{12,8},{13,9},{2,6},{3,7},{1... | collective-permute-start | bytes 2162696 | tf_op jit(solution)/shard_map/ppermute | solution.py:48
  56.6 25.2 %collective-permute-start.15 = (f32[16,88,128]{2,1,0:T(8,128)S(1)}, f32[16,88,128]{2,1,0:T(8,128)S(1)}, u32[]{:S(2)}, u32[]{:S(2)}) collective-permute-start(f32[16,88,128]{2,1,0:T(8,128)S(1)} %get-tuple-element.74), channel_id=1, source_target_pairs={{4,8},{5,9},{0,1},{12,13},{8,4},{9,5},{1,0},{13,12},{6,10},{7,11},... | collective-permute-start | bytes 2162696 | tf_op jit(solution)/shard_map/ppermute | solution.py:48
  56.6 20.5 %collective-permute-start.11 = (f32[16,40,128]{2,1,0:T(8,128)S(1)}, f32[16,40,128]{2,1,0:T(8,128)S(1)}, u32[]{:S(2)}, u32[]{:S(2)}) collective-permute-start(f32[16,40,128]{2,1,0:T(8,128)S(1)} %get-tuple-element.69), channel_id=1, source_target_pairs={{0,4},{1,5},{8,12},{9,13},{4,0},{5,1},{12,8},{13,9},{2,6},{3,7},{1... | collective-permute-start | bytes 983048 | tf_op jit(solution)/shard_map/ppermute | solution.py:48
  58.6 18.6 %collective-permute-start.12 = (f32[16,40,128]{2,1,0:T(8,128)S(1)}, f32[16,40,128]{2,1,0:T(8,128)S(1)}, u32[]{:S(2)}, u32[]{:S(2)}) collective-permute-start(f32[16,40,128]{2,1,0:T(8,128)S(1)} %get-tuple-element.70), channel_id=1, source_target_pairs={{4,8},{5,9},{0,1},{12,13},{8,4},{9,5},{1,0},{13,12},{6,10},{7,11},... | collective-permute-start | bytes 983048 | tf_op jit(solution)/shard_map/ppermute | solution.py:48
  63.4 18.4 %collective-permute-start.16 = (f32[4,88,128]{2,1,0:T(8,128)S(1)}, f32[4,88,128]{2,1,0:T(8,128)S(1)}, u32[]{:S(2)}, u32[]{:S(2)}) collective-permute-start(f32[4,88,128]{2,1,0:T(8,128)S(1)} %get-tuple-element.75), channel_id=1, source_target_pairs={{0,16},{1,17},{16,0},{17,1},{2,18},{3,19},{18,2},{19,3},{4,20},{5,... | collective-permute-start | bytes 540680 | tf_op jit(solution)/shard_map/ppermute | solution.py:48
  83.2 33.9 %collective-permute-start.29 = (f32[16,88,128]{2,1,0:T(8,128)S(1)}, f32[16,88,128]{2,1,0:T(8,128)S(1)}, u32[]{:S(2)}, u32[]{:S(2)}) collective-permute-start(f32[16,88,128]{2,1,0:T(8,128)S(1)} %get-tuple-element.92), channel_id=1, source_target_pairs={{0,4},{1,5},{8,12},{9,13},{4,0},{5,1},{12,8},{13,9},{2,6},{3,7},{1... | collective-permute-start | bytes 2162696 | tf_op jit(solution)/shard_map/ppermute | solution.py:48
  85.0 32.1 %collective-permute-start.30 = (f32[16,88,128]{2,1,0:T(8,128)S(1)}, f32[16,88,128]{2,1,0:T(8,128)S(1)}, u32[]{:S(2)}, u32[]{:S(2)}) collective-permute-start(f32[16,88,128]{2,1,0:T(8,128)S(1)} %get-tuple-element.93), channel_id=1, source_target_pairs={{4,8},{5,9},{0,1},{12,13},{8,4},{9,5},{1,0},{13,12},{6,10},{7,11},... | collective-permute-start | bytes 2162696 | tf_op jit(solution)/shard_map/ppermute | solution.py:48
  85.0 19.6 %collective-permute-start.18 = (f32[16,40,128]{2,1,0:T(8,128)S(1)}, f32[16,40,128]{2,1,0:T(8,128)S(1)}, u32[]{:S(2)}, u32[]{:S(2)}) collective-permute-start(f32[16,40,128]{2,1,0:T(8,128)S(1)} %get-tuple-element.78), channel_id=1, source_target_pairs={{0,4},{1,5},{8,12},{9,13},{4,0},{5,1},{12,8},{13,9},{2,6},{3,7},{1... | collective-permute-start | bytes 983048 | tf_op jit(solution)/shard_map/ppermute | solution.py:48
  86.7 17.9 %collective-permute-start.19 = (f32[16,40,128]{2,1,0:T(8,128)S(1)}, f32[16,40,128]{2,1,0:T(8,128)S(1)}, u32[]{:S(2)}, u32[]{:S(2)}) collective-permute-start(f32[16,40,128]{2,1,0:T(8,128)S(1)} %get-tuple-element.79), channel_id=1, source_target_pairs={{4,8},{5,9},{0,1},{12,13},{8,4},{9,5},{1,0},{13,12},{6,10},{7,11},... | collective-permute-start | bytes 983048 | tf_op jit(solution)/shard_map/ppermute | solution.py:48
  91.6 22.5 %collective-permute-start.31 = (f32[4,88,128]{2,1,0:T(8,128)S(1)}, f32[4,88,128]{2,1,0:T(8,128)S(1)}, u32[]{:S(2)}, u32[]{:S(2)}) collective-permute-start(f32[4,88,128]{2,1,0:T(8,128)S(1)} %get-tuple-element.94), channel_id=1, source_target_pairs={{0,16},{1,17},{16,0},{17,1},{2,18},{3,19},{18,2},{19,3},{4,20},{5,... | collective-permute-start | bytes 540680 | tf_op jit(solution)/shard_map/ppermute | solution.py:48
  107.8 15.0 %collective-permute-start.21 = (f32[16,24,128]{2,1,0:T(8,128)S(1)}, f32[16,24,128]{2,1,0:T(8,128)S(1)}, u32[]{:S(2)}, u32[]{:S(2)}) collective-permute-start(f32[16,24,128]{2,1,0:T(8,128)S(1)} %get-tuple-element.82), channel_id=1, source_target_pairs={{0,4},{1,5},{8,12},{9,13},{4,0},{5,1},{12,8},{13,9},{2,6},{3,7},{1... | collective-permute-start | bytes 589832 | tf_op jit(solution)/shard_map/ppermute | solution.py:48
  115.5 11.7 %collective-permute-start.33 = (f32[2,2,128,128]{3,2,1,0:T(8,128)S(1)}, f32[2,2,128,128]{3,2,1,0:T(8,128)S(1)}, u32[]{:S(2)}, u32[]{:S(2)}) collective-permute-start(f32[2,2,128,128]{3,2,1,0:T(8,128)S(1)} %get-tuple-element.98.refs_1_), channel_id=1, source_target_pairs={{0,16},{16,0},{1,17},{17,1},{2,18},{18,2},{3,19},{19,3},{4,20},{20... | collective-permute-start | bytes 786440 | tf_op jit(solution)/shard_map/ppermute | solution.py:372
  118.4 10.5 %collective-permute-start.32 = (f32[2,2,88,128]{3,2,1,0:T(8,128)S(1)}, f32[2,2,88,128]{3,2,1,0:T(8,128)S(1)}, u32[]{:S(2)}, u32[]{:S(2)}) collective-permute-start(f32[2,2,88,128]{3,2,1,0:T(8,128)S(1)} %get-tuple-element.97.refs_1_), channel_id=1, source_target_pairs={{0,16},{16,0},{1,17},{17,1},{2,18},{18,2},{3,19},{19,3},{4,20},{20... | collective-permute-start | bytes 540680 | tf_op jit(solution)/shard_map/ppermute | solution.py:372
  119.0 6.7 %collective-permute-start.26 = (f32[16,16,128]{2,1,0:T(8,128)S(1)}, f32[16,16,128]{2,1,0:T(8,128)S(1)}, u32[]{:S(2)}, u32[]{:S(2)}) collective-permute-start(f32[16,16,128]{2,1,0:T(8,128)S(1)} %get-tuple-element.88), channel_id=1, source_target_pairs={{0,4},{1,5},{8,12},{9,13},{4,0},{5,1},{12,8},{13,9},{2,6},{3,7},{1... | collective-permute-start | bytes 393224 | tf_op jit(solution)/shard_map/ppermute | solution.py:48
  123.1 7.5 %collective-permute-start.25 = (f32[2,2,24,128]{3,2,1,0:T(8,128)S(1)}, f32[2,2,24,128]{3,2,1,0:T(8,128)S(1)}, u32[]{:S(2)}, u32[]{:S(2)}) collective-permute-start(f32[2,2,24,128]{3,2,1,0:T(8,128)S(1)} %get-tuple-element.87.refs_1_), channel_id=1, source_target_pairs={{0,16},{16,0},{1,17},{17,1},{2,18},{18,2},{3,19},{19,3},{4,20},{20... | collective-permute-start | bytes 147464 | tf_op jit(solution)/shard_map/ppermute | solution.py:372
  (10 other events, 44.7 us)

commit v3 on v2

--- a/solution.py
+++ b/solution.py
@@ -8,7 +8,7 @@
 
 STEPS = 4
 CHUNKS = (11, 5)
-LAST_CUT = (3, 2)
+LAST_CUT = (4, 1)
 ROWS = 8
 HBM = pl.BlockSpec(memory_space=pltpu.HBM)
 VMEM = pl.BlockSpec(memory_space=pltpu.VMEM)
@@ -302,32 +302,34 @@
     return new, z, y, outs
 
 
-def finish(jobs, anomaly, field, shape):
+def finish(jobs, finished, anomaly, field, shape):
     J, _, _, L = shape
     buffers = [buffer for buffer in (anomaly, field) if buffer is not None]
     outs_count = 1 if field is None else 2
     ins, scratch = [], []
     for new, own, others, layers, (k0, kc) in jobs:
         ins += [new, own] + list(others)
-        scratch += [pltpu.VMEM((J, len(layers), kc, L), F32), pltpu.SemaphoreType.DMA((2, len(layers)))]
+        scratch += [pltpu.VMEM((J, len(layers), kc, L), F32), pltpu.SemaphoreType.DMA((len(layers),))]
+    ins += [job[0] for job in finished]
+    scratch += [pltpu.SemaphoreType.DMA((len(job[3]),)) for job in finished]
 
     def body(*refs):
         refs = list(refs)
         cells = []
         for _, _, others, _, _ in jobs:
             cells.append((refs.pop(0), [refs.pop(0) for _ in range(1 + len(others))]))
+        written = [refs.pop(0) for _ in finished]
         for _ in buffers:
             refs.pop(0)
         outs = [refs.pop(0) for _ in range(outs_count)]
         copies = []
-        if field is not None:
-            for n, ((u, _), (*_, layers, (k0, kc))) in enumerate(zip(cells, jobs)):
-                copies += write_copies(u, outs[1], layers, k0, kc, refs[2 * n + 1].at[1])
-            for copy in copies:
-                copy.start()
+        for n, (u, (*_, layers, (k0, kc))) in enumerate(zip(written, finished)):
+            copies += write_copies(u, outs[1], layers, k0, kc, refs[2 * len(jobs) + n])
+        for copy in copies:
+            copy.start()
         for m, ((u, sums), (*_, layers, (k0, kc))) in enumerate(zip(cells, jobs)):
             scaled, sems = refs[2 * m], refs[2 * m + 1]
-            results = write_copies(scaled, outs[0], layers, k0, kc, sems.at[0])
+            results = write_copies(scaled, outs[0], layers, k0, kc, sems)
             for n in range(len(layers)):
 
                 def tile(t, carry, n=n, u=u, sums=sums, scaled=scaled):
@@ -443,9 +445,10 @@
         sums.append((new, own, others, layers, span))
     for n, group in enumerate(([sums[0]], [sums[1]], sums[2:])):
         if group:
-            done = finish(group, anomaly, field if n > 0 else None, shape)
+            finished = sums[1:] if n == 1 else []
+            done = finish(group, finished, anomaly, field if finished else None, shape)
             anomaly = done[0]
-            field = done[1] if n > 0 else field
+            field = done[1] if finished else field
     return anomaly, field
 
 

time: 132 us -> 129 us (0.977)
  starting transfers between devices: 45 us -> 41.2 us
    ppermute x30, starting transfers between devices: 40.3 us -> 37.2 us  [exchange(): lax.ppermute(buffer, (axis, 'trial'), pairs + [(b, a) for a, b in pairs])]
    ppermute x4, waiting for transfers between devices: 0.01 us -> 2.74 us  [other_rows(): lax.ppermute(own, 'rows', [(i, (i + shift) % count) for i in range(count)])]
    ppermute x30, waiting for transfers between devices: 64.1 us -> 62.2 us  [exchange(): lax.ppermute(buffer, (axis, 'trial'), pairs + [(b, a) for a, b in pairs])]
  transfers between devices with their start and end apart: 34 -> 34, of which waited for: 12 -> 13; matrix products, arithmetic and copies ran while one was open for 0% -> 0% of each run, Pallas kernels for 11% -> 12%
where the time goes in v3:
time: 129 us
  waiting for transfers between devices  64.9 us (50%)
  starting transfers between devices  41.2 us (32%)
  Pallas kernels  22 us (17%)
    ppermute x30, waiting for transfers between devices, exchange(): lax.ppermute(buffer, (axis, 'trial'), pairs + [(b, a) for a, b in pairs])  62.2 us
    ppermute x30, starting transfers between devices, exchange(): lax.ppermute(buffer, (axis, 'trial'), pairs + [(b, a) for a, b in pairs])  37.2 us
    pallas_call x16, Pallas kernels, call(): pl.pallas_call(body, in_specs=in_specs, out_shape=outs, out_specs=out_spe...  22 us
    ppermute x4, starting transfers between devices, other_rows(): lax.ppermute(own, 'rows', [(i, (i + shift) % count) for i in range(count)])  4.06 us
    ppermute x4, waiting for transfers between devices, other_rows(): lax.ppermute(own, 'rows', [(i, (i + shift) % count) for i in range(count)])  2.74 us
  transfers between devices with their start and end apart: 34, of which 13 were waited for; matrix products, arithmetic and copies ran while one was open for 0% of the time, Pallas kernels for 12%

profile of v3, /device:TPU:0, one launch (start us, length us, event | category | flops | bytes accessed | tf_op | source)
XLA Modules:
  0.0 129.0 jit_solution(4314038422533872479)
XLA Ops:
  2.0 3.1 %collective-permute-start = (f32[16,88,128]{2,1,0:T(8,128)S(1)}, f32[16,88,128]{2,1,0:T(8,128)S(1)}, u32[]{:S(2)}, u32[]{:S(2)}) collective-permute-start(f32[16,88,128]{2,1,0:T(8,128)S(1)} %get-tuple-element.55), channel_id=1, source_target_pairs={{0,4},{1,5},{8,12},{9,13},{4,0},{5,1},{12,8},{13,9},{2,6},{3,7},{1... | collective-permute-start | bytes 2162696 | tf_op jit(solution)/shard_map/ppermute | solution.py:48
  6.3 1.6 %collective-permute-start.2 = (f32[4,88,128]{2,1,0:T(8,128)S(1)}, f32[4,88,128]{2,1,0:T(8,128)S(1)}, u32[]{:S(2)}, u32[]{:S(2)}) collective-permute-start(f32[4,88,128]{2,1,0:T(8,128)S(1)} %get-tuple-element.57), channel_id=1, source_target_pairs={{0,16},{1,17},{16,0},{17,1},{2,18},{3,19},{18,2},{19,3},{4,20},{5,... | collective-permute-start | bytes 540680 | tf_op jit(solution)/shard_map/ppermute | solution.py:48
  9.4 4.7 %shard_map.50 = (f32[16,4,128,128]{3,2,1,0:T(8,128)S(1)}, f32[16,4,128,128]{3,2,1,0:T(8,128)S(1)}, f32[16,4,128,128]{3,2,1,0:T(8,128)S(1)}) custom-call(f32[16,4,128,128]{3,2,1,0:T(8,128)} %u.3, f32[16,4,128,128]{3,2,1,0:T(8,128)} %refs_1_.1, f32[16,4,128,128]{3,2,1,0:T(8,128)} %refs_2_.1), custom_call_target="tpu_custom_call" | custom-call | tf_op jit(solution)/shard_map/pallas_call | solution.py:23
  14.1 7.2 %collective-permute-done.refs_3_ = f32[16,88,128]{2,1,0:T(8,128)S(1)} collective-permute-done((f32[16,88,128]{2,1,0:T(8,128)S(1)}, f32[16,88,128]{2,1,0:T(8,128)S(1)}, u32[]{:S(2)}, u32[]{:S(2)}) %collective-permute-start) | collective-permute-done | bytes 720928 | tf_op jit(solution)/shard_map/ppermute | solution.py:48
  21.3 2.0 %shard_map.53 = (f32[16,4,88,128]{3,2,1,0:T(8,128)S(1)}, f32[16,88,128]{2,1,0:T(8,128)S(1)}, f32[16,88,128]{2,1,0:T(8,128)S(1)}, f32[4,88,128]{2,1,0:T(8,128)S(1)}) custom-call(f32[16,4,128,128]{3,2,1,0:T(8,128)S(1)} %get-tuple-element.52.refs_0_, f32[16,4,128,128]{3,2,1,0:T(8,128)S(1)} %get-tuple-element.53.refs_1_, ...), custom_call_target="tpu_custom_call" | custom-call | flops 7208960 | tf_op jit(solution)/shard_map/pallas_call | solution.py:23
  23.2 2.9 %collective-permute-start.7 = (f32[16,88,128]{2,1,0:T(8,128)S(1)}, f32[16,88,128]{2,1,0:T(8,128)S(1)}, u32[]{:S(2)}, u32[]{:S(2)}) collective-permute-start(f32[16,88,128]{2,1,0:T(8,128)S(1)} %get-tuple-element.64), channel_id=1, source_target_pairs={{0,4},{1,5},{8,12},{9,13},{4,0},{5,1},{12,8},{13,9},{2,6},{3,7},{1... | collective-permute-start | bytes 2162696 | tf_op jit(solution)/shard_map/ppermute | solution.py:48
  26.2 2.0 %collective-permute-start.4 = (f32[16,40,128]{2,1,0:T(8,128)S(1)}, f32[16,40,128]{2,1,0:T(8,128)S(1)}, u32[]{:S(2)}, u32[]{:S(2)}) collective-permute-start(f32[16,40,128]{2,1,0:T(8,128)S(1)} %get-tuple-element.60), channel_id=1, source_target_pairs={{0,4},{1,5},{8,12},{9,13},{4,0},{5,1},{12,8},{13,9},{2,6},{3,7},{1... | collective-permute-start | bytes 983048 | tf_op jit(solution)/shard_map/ppermute | solution.py:48
  29.7 3.3 %collective-permute-done.6.refs_5_ = f32[4,40,128]{2,1,0:T(8,128)S(1)} collective-permute-done((f32[4,40,128]{2,1,0:T(8,128)S(1)}, f32[4,40,128]{2,1,0:T(8,128)S(1)}, u32[]{:S(2)}, u32[]{:S(2)}) %collective-permute-start.6) | collective-permute-done | bytes 81952 | tf_op jit(solution)/shard_map/ppermute | solution.py:48
  34.6 13.9 %collective-permute-done.4.refs_3_ = f32[16,40,128]{2,1,0:T(8,128)S(1)} collective-permute-done((f32[16,40,128]{2,1,0:T(8,128)S(1)}, f32[16,40,128]{2,1,0:T(8,128)S(1)}, u32[]{:S(2)}, u32[]{:S(2)}) %collective-permute-start.4) | collective-permute-done | bytes 327712 | tf_op jit(solution)/shard_map/ppermute | solution.py:48
  51.0 2.4 %collective-permute-done.10.refs_7_ = f32[16,4,128]{2,1,0:T(4,128)S(1)} collective-permute-done((f32[16,4,128]{2,1,0:T(4,128)S(1)}, f32[16,4,128]{2,1,0:T(4,128)S(1)}, u32[]{:S(2)}, u32[]{:S(2)}) %collective-permute-start.10) | collective-permute-done | bytes 32800 | tf_op jit(solution)/shard_map/ppermute | solution.py:48
  54.7 1.9 %collective-permute-start.14 = (f32[16,88,128]{2,1,0:T(8,128)S(1)}, f32[16,88,128]{2,1,0:T(8,128)S(1)}, u32[]{:S(2)}, u32[]{:S(2)}) collective-permute-start(f32[16,88,128]{2,1,0:T(8,128)S(1)} %get-tuple-element.73), channel_id=1, source_target_pairs={{0,4},{1,5},{8,12},{9,13},{4,0},{5,1},{12,8},{13,9},{2,6},{3,7},{1... | collective-permute-start | bytes 2162696 | tf_op jit(solution)/shard_map/ppermute | solution.py:48
  56.6 1.9 %collective-permute-start.11 = (f32[16,40,128]{2,1,0:T(8,128)S(1)}, f32[16,40,128]{2,1,0:T(8,128)S(1)}, u32[]{:S(2)}, u32[]{:S(2)}) collective-permute-start(f32[16,40,128]{2,1,0:T(8,128)S(1)} %get-tuple-element.69), channel_id=1, source_target_pairs={{0,4},{1,5},{8,12},{9,13},{4,0},{5,1},{12,8},{13,9},{2,6},{3,7},{1... | collective-permute-start | bytes 983048 | tf_op jit(solution)/shard_map/ppermute | solution.py:48
  60.1 3.3 %collective-permute-done.13.refs_6_ = f32[4,40,128]{2,1,0:T(8,128)S(1)} collective-permute-done((f32[4,40,128]{2,1,0:T(8,128)S(1)}, f32[4,40,128]{2,1,0:T(8,128)S(1)}, u32[]{:S(2)}, u32[]{:S(2)}) %collective-permute-start.13) | collective-permute-done | bytes 81952 | tf_op jit(solution)/shard_map/ppermute | solution.py:48
  65.0 12.2 %collective-permute-done.11.refs_4_ = f32[16,40,128]{2,1,0:T(8,128)S(1)} collective-permute-done((f32[16,40,128]{2,1,0:T(8,128)S(1)}, f32[16,40,128]{2,1,0:T(8,128)S(1)}, u32[]{:S(2)}, u32[]{:S(2)}) %collective-permute-start.11) | collective-permute-done | bytes 327712 | tf_op jit(solution)/shard_map/ppermute | solution.py:48
  79.4 2.4 %collective-permute-done.17.refs_7_ = f32[16,4,128]{2,1,0:T(4,128)S(1)} collective-permute-done((f32[16,4,128]{2,1,0:T(4,128)S(1)}, f32[16,4,128]{2,1,0:T(4,128)S(1)}, u32[]{:S(2)}, u32[]{:S(2)}) %collective-permute-start.17) | collective-permute-done | bytes 32800 | tf_op jit(solution)/shard_map/ppermute | solution.py:48
  83.2 1.8 %collective-permute-start.29 = (f32[16,88,128]{2,1,0:T(8,128)S(1)}, f32[16,88,128]{2,1,0:T(8,128)S(1)}, u32[]{:S(2)}, u32[]{:S(2)}) collective-permute-start(f32[16,88,128]{2,1,0:T(8,128)S(1)} %get-tuple-element.92), channel_id=1, source_target_pairs={{0,4},{1,5},{8,12},{9,13},{4,0},{5,1},{12,8},{13,9},{2,6},{3,7},{1... | collective-permute-start | bytes 2162696 | tf_op jit(solution)/shard_map/ppermute | solution.py:48
  85.0 1.7 %collective-permute-start.18 = (f32[16,40,128]{2,1,0:T(8,128)S(1)}, f32[16,40,128]{2,1,0:T(8,128)S(1)}, u32[]{:S(2)}, u32[]{:S(2)}) collective-permute-start(f32[16,40,128]{2,1,0:T(8,128)S(1)} %get-tuple-element.78), channel_id=1, source_target_pairs={{0,4},{1,5},{8,12},{9,13},{4,0},{5,1},{12,8},{13,9},{2,6},{3,7},{1... | collective-permute-start | bytes 983048 | tf_op jit(solution)/shard_map/ppermute | solution.py:48
  88.2 3.3 %collective-permute-done.20.refs_6_ = f32[4,40,128]{2,1,0:T(8,128)S(1)} collective-permute-done((f32[4,40,128]{2,1,0:T(8,128)S(1)}, f32[4,40,128]{2,1,0:T(8,128)S(1)}, u32[]{:S(2)}, u32[]{:S(2)}) %collective-permute-start.20) | collective-permute-done | bytes 81952 | tf_op jit(solution)/shard_map/ppermute | solution.py:48
  93.1 10.6 %collective-permute-done.18.refs_4_ = f32[16,40,128]{2,1,0:T(8,128)S(1)} collective-permute-done((f32[16,40,128]{2,1,0:T(8,128)S(1)}, f32[16,40,128]{2,1,0:T(8,128)S(1)}, u32[]{:S(2)}, u32[]{:S(2)}) %collective-permute-start.18) | collective-permute-done | bytes 327712 | tf_op jit(solution)/shard_map/ppermute | solution.py:48
  107.5 2.4 %collective-permute-done.24.refs_7_.refs_6_ = f32[16,4,128]{2,1,0:T(4,128)S(1)} collective-permute-done((f32[16,4,128]{2,1,0:T(4,128)S(1)}, f32[16,4,128]{2,1,0:T(4,128)S(1)}, u32[]{:S(2)}, u32[]{:S(2)}) %collective-permute-start.24) | collective-permute-done | bytes 32800 | tf_op jit(solution)/shard_map/ppermute | solution.py:48
  109.9 1.7 %collective-permute-start.21 = (f32[16,32,128]{2,1,0:T(8,128)S(1)}, f32[16,32,128]{2,1,0:T(8,128)S(1)}, u32[]{:S(2)}, u32[]{:S(2)}) collective-permute-start(f32[16,32,128]{2,1,0:T(8,128)S(1)} %get-tuple-element.82), channel_id=1, source_target_pairs={{0,4},{1,5},{8,12},{9,13},{4,0},{5,1},{12,8},{13,9},{2,6},{3,7},{1... | collective-permute-start | bytes 786440 | tf_op jit(solution)/shard_map/ppermute | solution.py:48
  122.3 1.7 %shard_map.63.refs_6_ = f32[16,4,128,128]{3,2,1,0:T(8,128)} custom-call(f32[16,2,128,128]{3,2,1,0:T(8,128)S(1)} %get-tuple-element.95.refs_8_.refs_0_, f32[2,2,128,128]{3,2,1,0:T(8,128)S(1)} %get-tuple-element.98.refs_1_, f32[2,2,128,128]{3,2,1,0:T(8,128)S(1)} %collective-permute-done.33.refs_2_), custom_call_target="tpu_custom_call" | custom-call | flops 5242880 | tf_op jit(solution)/shard_map/pallas_call | solution.py:23
  124.0 2.1 %collective-permute-done.32.refs_2_ = f32[2,2,88,128]{3,2,1,0:T(8,128)S(1)} collective-permute-done((f32[2,2,88,128]{3,2,1,0:T(8,128)S(1)}, f32[2,2,88,128]{3,2,1,0:T(8,128)S(1)}, u32[]{:S(2)}, u32[]{:S(2)}) %collective-permute-start.32) | collective-permute-done | bytes 180256 | tf_op jit(solution)/shard_map/ppermute | solution.py:374
  126.1 1.9 %shard_map.64 = (f32[16,4,128,128]{3,2,1,0:T(8,128)}, f32[16,4,128,128]{3,2,1,0:T(8,128)}) custom-call(f32[16,2,88,128]{3,2,1,0:T(8,128)S(1)} %get-tuple-element.96.refs_0_.refs_3_, f32[2,2,88,128]{3,2,1,0:T(8,128)S(1)} %get-tuple-element.97.refs_1_, ...), custom_call_target="tpu_custom_call", output_to_operand_aliasing={{0}: (6, {}), {1}: (7, {})} | custom-call | flops 3604480 | tf_op jit(solution)/shard_map/pallas_call | solution.py:23
  (60 shorter events, 35.9 us)
Async XLA Ops:
  2.0 19.3 %collective-permute-start = (f32[16,88,128]{2,1,0:T(8,128)S(1)}, f32[16,88,128]{2,1,0:T(8,128)S(1)}, u32[]{:S(2)}, u32[]{:S(2)}) collective-permute-start(f32[16,88,128]{2,1,0:T(8,128)S(1)} %get-tuple-element.55), channel_id=1, source_target_pairs={{0,4},{1,5},{8,12},{9,13},{4,0},{5,1},{12,8},{13,9},{2,6},{3,7},{1... | collective-permute-start | bytes 2162696 | tf_op jit(solution)/shard_map/ppermute | solution.py:48
  5.1 16.1 %collective-permute-start.1 = (f32[16,88,128]{2,1,0:T(8,128)S(1)}, f32[16,88,128]{2,1,0:T(8,128)S(1)}, u32[]{:S(2)}, u32[]{:S(2)}) collective-permute-start(f32[16,88,128]{2,1,0:T(8,128)S(1)} %get-tuple-element.56), channel_id=1, source_target_pairs={{4,8},{5,9},{0,1},{12,13},{8,4},{9,5},{1,0},{13,12},{6,10},{7,11},... | collective-permute-start | bytes 2162696 | tf_op jit(solution)/shard_map/ppermute | solution.py:48
  6.3 7.8 %collective-permute-start.2 = (f32[4,88,128]{2,1,0:T(8,128)S(1)}, f32[4,88,128]{2,1,0:T(8,128)S(1)}, u32[]{:S(2)}, u32[]{:S(2)}) collective-permute-start(f32[4,88,128]{2,1,0:T(8,128)S(1)} %get-tuple-element.57), channel_id=1, source_target_pairs={{0,16},{1,17},{16,0},{17,1},{2,18},{3,19},{18,2},{19,3},{4,20},{5,... | collective-permute-start | bytes 540680 | tf_op jit(solution)/shard_map/ppermute | solution.py:48
  23.2 30.2 %collective-permute-start.7 = (f32[16,88,128]{2,1,0:T(8,128)S(1)}, f32[16,88,128]{2,1,0:T(8,128)S(1)}, u32[]{:S(2)}, u32[]{:S(2)}) collective-permute-start(f32[16,88,128]{2,1,0:T(8,128)S(1)} %get-tuple-element.64), channel_id=1, source_target_pairs={{0,4},{1,5},{8,12},{9,13},{4,0},{5,1},{12,8},{13,9},{2,6},{3,7},{1... | collective-permute-start | bytes 2162696 | tf_op jit(solution)/shard_map/ppermute | solution.py:48
  26.2 27.2 %collective-permute-start.8 = (f32[16,88,128]{2,1,0:T(8,128)S(1)}, f32[16,88,128]{2,1,0:T(8,128)S(1)}, u32[]{:S(2)}, u32[]{:S(2)}) collective-permute-start(f32[16,88,128]{2,1,0:T(8,128)S(1)} %get-tuple-element.65), channel_id=1, source_target_pairs={{4,8},{5,9},{0,1},{12,13},{8,4},{9,5},{1,0},{13,12},{6,10},{7,11},... | collective-permute-start | bytes 2162696 | tf_op jit(solution)/shard_map/ppermute | solution.py:48
  26.2 22.3 %collective-permute-start.4 = (f32[16,40,128]{2,1,0:T(8,128)S(1)}, f32[16,40,128]{2,1,0:T(8,128)S(1)}, u32[]{:S(2)}, u32[]{:S(2)}) collective-permute-start(f32[16,40,128]{2,1,0:T(8,128)S(1)} %get-tuple-element.60), channel_id=1, source_target_pairs={{0,4},{1,5},{8,12},{9,13},{4,0},{5,1},{12,8},{13,9},{2,6},{3,7},{1... | collective-permute-start | bytes 983048 | tf_op jit(solution)/shard_map/ppermute | solution.py:48
  28.2 20.3 %collective-permute-start.5 = (f32[16,40,128]{2,1,0:T(8,128)S(1)}, f32[16,40,128]{2,1,0:T(8,128)S(1)}, u32[]{:S(2)}, u32[]{:S(2)}) collective-permute-start(f32[16,40,128]{2,1,0:T(8,128)S(1)} %get-tuple-element.61), channel_id=1, source_target_pairs={{4,8},{5,9},{0,1},{12,13},{8,4},{9,5},{1,0},{13,12},{6,10},{7,11},... | collective-permute-start | bytes 983048 | tf_op jit(solution)/shard_map/ppermute | solution.py:48
  33.1 20.4 %collective-permute-start.9 = (f32[4,88,128]{2,1,0:T(8,128)S(1)}, f32[4,88,128]{2,1,0:T(8,128)S(1)}, u32[]{:S(2)}, u32[]{:S(2)}) collective-permute-start(f32[4,88,128]{2,1,0:T(8,128)S(1)} %get-tuple-element.66), channel_id=1, source_target_pairs={{0,16},{1,17},{16,0},{17,1},{2,18},{3,19},{18,2},{19,3},{4,20},{5,... | collective-permute-start | bytes 540680 | tf_op jit(solution)/shard_map/ppermute | solution.py:48
  54.7 27.1 %collective-permute-start.14 = (f32[16,88,128]{2,1,0:T(8,128)S(1)}, f32[16,88,128]{2,1,0:T(8,128)S(1)}, u32[]{:S(2)}, u32[]{:S(2)}) collective-permute-start(f32[16,88,128]{2,1,0:T(8,128)S(1)} %get-tuple-element.73), channel_id=1, source_target_pairs={{0,4},{1,5},{8,12},{9,13},{4,0},{5,1},{12,8},{13,9},{2,6},{3,7},{1... | collective-permute-start | bytes 2162696 | tf_op jit(solution)/shard_map/ppermute | solution.py:48
  56.6 25.2 %collective-permute-start.15 = (f32[16,88,128]{2,1,0:T(8,128)S(1)}, f32[16,88,128]{2,1,0:T(8,128)S(1)}, u32[]{:S(2)}, u32[]{:S(2)}) collective-permute-start(f32[16,88,128]{2,1,0:T(8,128)S(1)} %get-tuple-element.74), channel_id=1, source_target_pairs={{4,8},{5,9},{0,1},{12,13},{8,4},{9,5},{1,0},{13,12},{6,10},{7,11},... | collective-permute-start | bytes 2162696 | tf_op jit(solution)/shard_map/ppermute | solution.py:48
  56.6 20.5 %collective-permute-start.11 = (f32[16,40,128]{2,1,0:T(8,128)S(1)}, f32[16,40,128]{2,1,0:T(8,128)S(1)}, u32[]{:S(2)}, u32[]{:S(2)}) collective-permute-start(f32[16,40,128]{2,1,0:T(8,128)S(1)} %get-tuple-element.69), channel_id=1, source_target_pairs={{0,4},{1,5},{8,12},{9,13},{4,0},{5,1},{12,8},{13,9},{2,6},{3,7},{1... | collective-permute-start | bytes 983048 | tf_op jit(solution)/shard_map/ppermute | solution.py:48
  58.6 18.6 %collective-permute-start.12 = (f32[16,40,128]{2,1,0:T(8,128)S(1)}, f32[16,40,128]{2,1,0:T(8,128)S(1)}, u32[]{:S(2)}, u32[]{:S(2)}) collective-permute-start(f32[16,40,128]{2,1,0:T(8,128)S(1)} %get-tuple-element.70), channel_id=1, source_target_pairs={{4,8},{5,9},{0,1},{12,13},{8,4},{9,5},{1,0},{13,12},{6,10},{7,11},... | collective-permute-start | bytes 983048 | tf_op jit(solution)/shard_map/ppermute | solution.py:48
  63.4 18.4 %collective-permute-start.16 = (f32[4,88,128]{2,1,0:T(8,128)S(1)}, f32[4,88,128]{2,1,0:T(8,128)S(1)}, u32[]{:S(2)}, u32[]{:S(2)}) collective-permute-start(f32[4,88,128]{2,1,0:T(8,128)S(1)} %get-tuple-element.75), channel_id=1, source_target_pairs={{0,16},{1,17},{16,0},{17,1},{2,18},{3,19},{18,2},{19,3},{4,20},{5,... | collective-permute-start | bytes 540680 | tf_op jit(solution)/shard_map/ppermute | solution.py:48
  83.2 30.4 %collective-permute-start.29 = (f32[16,88,128]{2,1,0:T(8,128)S(1)}, f32[16,88,128]{2,1,0:T(8,128)S(1)}, u32[]{:S(2)}, u32[]{:S(2)}) collective-permute-start(f32[16,88,128]{2,1,0:T(8,128)S(1)} %get-tuple-element.92), channel_id=1, source_target_pairs={{0,4},{1,5},{8,12},{9,13},{4,0},{5,1},{12,8},{13,9},{2,6},{3,7},{1... | collective-permute-start | bytes 2162696 | tf_op jit(solution)/shard_map/ppermute | solution.py:48
  85.0 28.6 %collective-permute-start.30 = (f32[16,88,128]{2,1,0:T(8,128)S(1)}, f32[16,88,128]{2,1,0:T(8,128)S(1)}, u32[]{:S(2)}, u32[]{:S(2)}) collective-permute-start(f32[16,88,128]{2,1,0:T(8,128)S(1)} %get-tuple-element.93), channel_id=1, source_target_pairs={{4,8},{5,9},{0,1},{12,13},{8,4},{9,5},{1,0},{13,12},{6,10},{7,11},... | collective-permute-start | bytes 2162696 | tf_op jit(solution)/shard_map/ppermute | solution.py:48
  85.0 18.7 %collective-permute-start.18 = (f32[16,40,128]{2,1,0:T(8,128)S(1)}, f32[16,40,128]{2,1,0:T(8,128)S(1)}, u32[]{:S(2)}, u32[]{:S(2)}) collective-permute-start(f32[16,40,128]{2,1,0:T(8,128)S(1)} %get-tuple-element.78), channel_id=1, source_target_pairs={{0,4},{1,5},{8,12},{9,13},{4,0},{5,1},{12,8},{13,9},{2,6},{3,7},{1... | collective-permute-start | bytes 983048 | tf_op jit(solution)/shard_map/ppermute | solution.py:48
  86.7 17.0 %collective-permute-start.19 = (f32[16,40,128]{2,1,0:T(8,128)S(1)}, f32[16,40,128]{2,1,0:T(8,128)S(1)}, u32[]{:S(2)}, u32[]{:S(2)}) collective-permute-start(f32[16,40,128]{2,1,0:T(8,128)S(1)} %get-tuple-element.79), channel_id=1, source_target_pairs={{4,8},{5,9},{0,1},{12,13},{8,4},{9,5},{1,0},{13,12},{6,10},{7,11},... | collective-permute-start | bytes 983048 | tf_op jit(solution)/shard_map/ppermute | solution.py:48
  91.6 20.1 %collective-permute-start.31 = (f32[4,88,128]{2,1,0:T(8,128)S(1)}, f32[4,88,128]{2,1,0:T(8,128)S(1)}, u32[]{:S(2)}, u32[]{:S(2)}) collective-permute-start(f32[4,88,128]{2,1,0:T(8,128)S(1)} %get-tuple-element.94), channel_id=1, source_target_pairs={{0,16},{1,17},{16,0},{17,1},{2,18},{3,19},{18,2},{19,3},{4,20},{5,... | collective-permute-start | bytes 540680 | tf_op jit(solution)/shard_map/ppermute | solution.py:48
  104.4 7.2 %collective-permute-start.23 = (f32[4,40,128]{2,1,0:T(8,128)S(1)}, f32[4,40,128]{2,1,0:T(8,128)S(1)}, u32[]{:S(2)}, u32[]{:S(2)}) collective-permute-start(f32[4,40,128]{2,1,0:T(8,128)S(1)} %get-tuple-element.84), channel_id=1, source_target_pairs={{0,16},{1,17},{16,0},{17,1},{2,18},{3,19},{18,2},{19,3},{4,20},{5,... | collective-permute-start | bytes 245768 | tf_op jit(solution)/shard_map/ppermute | solution.py:48
  109.9 8.2 %collective-permute-start.21 = (f32[16,32,128]{2,1,0:T(8,128)S(1)}, f32[16,32,128]{2,1,0:T(8,128)S(1)}, u32[]{:S(2)}, u32[]{:S(2)}) collective-permute-start(f32[16,32,128]{2,1,0:T(8,128)S(1)} %get-tuple-element.82), channel_id=1, source_target_pairs={{0,4},{1,5},{8,12},{9,13},{4,0},{5,1},{12,8},{13,9},{2,6},{3,7},{1... | collective-permute-start | bytes 786440 | tf_op jit(solution)/shard_map/ppermute | solution.py:48
  113.0 9.2 %collective-permute-start.33 = (f32[2,2,128,128]{3,2,1,0:T(8,128)S(1)}, f32[2,2,128,128]{3,2,1,0:T(8,128)S(1)}, u32[]{:S(2)}, u32[]{:S(2)}) collective-permute-start(f32[2,2,128,128]{3,2,1,0:T(8,128)S(1)} %get-tuple-element.98.refs_1_), channel_id=1, source_target_pairs={{0,16},{16,0},{1,17},{17,1},{2,18},{18,2},{3,19},{19,3},{4,20},{20... | collective-permute-start | bytes 786440 | tf_op jit(solution)/shard_map/ppermute | solution.py:374
  114.9 11.2 %collective-permute-start.32 = (f32[2,2,88,128]{3,2,1,0:T(8,128)S(1)}, f32[2,2,88,128]{3,2,1,0:T(8,128)S(1)}, u32[]{:S(2)}, u32[]{:S(2)}) collective-permute-start(f32[2,2,88,128]{3,2,1,0:T(8,128)S(1)} %get-tuple-element.97.refs_1_), channel_id=1, source_target_pairs={{0,16},{16,0},{1,17},{17,1},{2,18},{18,2},{3,19},{19,3},{4,20},{20... | collective-permute-start | bytes 540680 | tf_op jit(solution)/shard_map/ppermute | solution.py:374
  118.6 9.4 %collective-permute-start.25 = (f32[2,2,32,128]{3,2,1,0:T(8,128)S(1)}, f32[2,2,32,128]{3,2,1,0:T(8,128)S(1)}, u32[]{:S(2)}, u32[]{:S(2)}) collective-permute-start(f32[2,2,32,128]{3,2,1,0:T(8,128)S(1)} %get-tuple-element.87.refs_1_), channel_id=1, source_target_pairs={{0,16},{16,0},{1,17},{17,1},{2,18},{18,2},{3,19},{19,3},{4,20},{20... | collective-permute-start | bytes 196616 | tf_op jit(solution)/shard_map/ppermute | solution.py:374
  120.9 7.1 %collective-permute-start.28 = (f32[2,2,8,128]{3,2,1,0:T(8,128)S(1)}, f32[2,2,8,128]{3,2,1,0:T(8,128)S(1)}, u32[]{:S(2)}, u32[]{:S(2)}) collective-permute-start(f32[2,2,8,128]{3,2,1,0:T(8,128)S(1)} %get-tuple-element.91.refs_4_), channel_id=1, source_target_pairs={{0,16},{16,0},{1,17},{17,1},{2,18},{18,2},{3,19},{19,3},{4,20},{20... | collective-permute-start | bytes 49160 | tf_op jit(solution)/shard_map/ppermute | solution.py:374
  (10 other events, 46.0 us)
